TPU v7x, 128 devices: a whole 4x4x4 slice. The times are simulated.
128 devices in a mesh: sub: 32 (over z, y, core), blk: 4 (over x).
Axes of the slice: x: 4, y: 4, z: 4, core: 2. Of those that a mesh axis runs over, the one named last changes fastest.
Arguments:
- initial_state: float32 [32, 64, 2048], P('sub', None, 'blk'), may hold values from -6 to 6
- source: bfloat16 [32, 8, 64, 2048], P('sub', None, None, 'blk'), may hold values from -6 to 6
- inverse_diag: float32 [32, 2048], P('sub', 'blk'), may hold values from 0.5 to 0.85
- inverse_off: bfloat16 [32, 2048, 2048], P('sub', None, 'blk'), may hold values from -0.032958984 to 0.032958984
- coupling: float32 [32, 128], P('sub', 'blk'), may hold values from 0.3 to 3
- initial_waves: bfloat16 [32, 128, 512], P('sub', 'blk'), may hold values from -6 to 6
- bucket: int32 [32], P('sub'), may hold values from 0 to 2
- partner: int32 [32, 128], P('sub', 'blk'), may hold values from 0 to 31
- position_of: int32 [32], replicated, may hold values from 0 to 31, each once
Outputs:
- last_state: float32 [32, 64, 2048], P('sub', None, 'blk')
- waveform: float32 [32, 128, 512], P('sub', 'blk')
Inputs may be any that keep to these rules, and one draw needn't show every extreme that they name: A subcircuit of bucket b takes 8 / 2 ** (2 - b) implicit Euler steps. `position_of`: a permutation.
All inputs are finite; a program needn't handle non-finite values.
Results may differ from a plain program's by a relative error of at most 0.0052.
Values may be sent and summed in bfloat16 or wider, within the bound.
No kernel may reach another device: no remote copies, remote signals or barrier semaphores. Data moves between devices by JAX's collectives and lax.ppermute only.
A program may use at most 64 MiB of HBM per device.

v0:
```python
import jax
import jax.numpy as jnp
from jax import lax
from jax.experimental import pallas as pl
from jax.experimental.pallas import tpu as pltpu
from jax.sharding import PartitionSpec as P


F32 = jnp.float32
BF16 = jnp.bfloat16
SLOTS = 4
FAR_ROWS = 1280
WIDE = 5


def hop(array, start, end):
    pairs = []
    for sub in range(32):
        home = 2 * (sub % 2)
        pairs.append((sub * 4 + (home + start) % 4, sub * 4 + (home + end) % 4))
    return lax.ppermute(array, ("sub", "blk"), pairs)


def to_home(array):
    return array, *(hop(array, d, 0) for d in (1, 2, 3))


def turn(array):
    parts = [array]
    for d in (1, 2, 3):
        pairs = [(sub * 4 + (r + d) % 4, sub * 4 + r) for sub in range(32) for r in range(4)]
        parts.append(lax.ppermute(array, ("sub", "blk"), pairs))
    return tuple(parts)


def from_home(slots, rel):
    one, two, three = (hop(slots[d], 0, d) for d in (1, 2, 3))
    return jnp.where(
        rel == 0, slots[0], jnp.where(rel == 1, one, jnp.where(rel == 2, two, three))
    )


def gather_matrix(matrix):
    half = FAR_ROWS
    one, three = hop(matrix, 1, 0), hop(matrix, 3, 0)
    near1, near3 = hop(matrix[:half], 2, 1), hop(matrix[half:], 2, 3)
    upper, lower = hop(near1, 1, 0), hop(near3, 3, 0)
    return matrix, one, upper, lower, three


def port_rows(ports, nodes):
    stride = nodes // ports
    port_at = lax.broadcasted_iota(jnp.int32, (ports, nodes), 0) * stride
    node_at = lax.broadcasted_iota(jnp.int32, (ports, nodes), 1)
    return port_at == node_at


def port_columns(ports, nodes):
    stride = nodes // ports
    port_at = lax.broadcasted_iota(jnp.int32, (nodes, ports), 1) * stride
    node_at = lax.broadcasted_iota(jnp.int32, (nodes, ports), 0)
    return port_at == node_at


def times_matrix(operand, matrices, d):
    if d == 2:
        half = FAR_ROWS
        total = jnp.dot(operand[:, :half], matrices[2][...], preferred_element_type=F32)
        return total + jnp.dot(operand[:, half:], matrices[3][...], preferred_element_type=F32)
    matrix = matrices[{0: 0, 1: 1, 3: 4}[d]]
    return jnp.dot(operand[...], matrix[...], preferred_element_type=F32)


DIAG = 64
INJECT = 65


def sweep_kernel(meta, a0_in, a1_in, a2_in, a3_in, a4_in, s0_in, s1_in, s2_in, s3_in, m0, m1, m2, m3, w0, w1, w2, w3,
                 out, response_out, history_out, operand, state, forced, response, history,
                 sent, a0, a1, a2, a3, a4, s0, s1, s2, s3, arrived):
    steps, cases, block = s0.shape
    ports = w0.shape[0]
    all_ports = SLOTS * ports
    nodes = SLOTS * block
    count, spacing, place = meta[0], meta[1], meta[2]
    spacing_float = spacing.astype(F32)
    matrices, sources, miscs = (a0, a1, a2, a3, a4), (s0, s1, s2, s3), (m0, m1, m2, m3)
    inputs = (s0_in, s1_in, s2_in, s3_in, a0_in, a1_in, a2_in, a3_in, a4_in)
    loads = [
        pltpu.make_async_copy(here, there, arrived.at[i])
        for i, (here, there) in enumerate(zip(inputs, sources + matrices))
    ]
    for load in loads:
        load.start()
    marks = port_rows(all_ports, nodes)
    spread = jnp.where(marks, 1.0, 0.0).astype(BF16)
    waves = jnp.concatenate([w[...] for w in (w0, w1, w2, w3)], axis=0).astype(F32)
    waves = jnp.transpose(waves).astype(BF16)
    forced[...] = jnp.dot(waves, spread, preferred_element_type=F32).astype(BF16)
    state[...] = jnp.where(marks, 1.0, 0.0)

    def argument(current, fine, d):
        rows = pl.ds(pl.multiple_of(fine * cases, cases), cases)
        lanes = slice(d * block, (d + 1) * block)
        drive = miscs[d][INJECT : INJECT + 1, :] * forced[rows, lanes].astype(F32)
        return (current + spacing_float * (sources[d][fine].astype(F32) + drive)).astype(BF16)

    def spot(d):
        return pl.ds(pl.multiple_of(lax.rem(place + d, SLOTS) * block, block), block)

    for load in loads[:SLOTS]:
        load.wait()
    for d in range(SLOTS):
        operand[0, :cases, spot(d)] = argument(miscs[d][:cases, :], spacing - 1, d)
        operand[0, cases:, spot(d)] = spread[:, d * block : (d + 1) * block]

    def send(k):
        rows = pl.ds(pl.multiple_of(k * all_ports, all_ports), all_ports)
        held = pl.ds(pl.multiple_of(k * cases, cases), cases)
        return (
            pltpu.make_async_copy(response.at[rows, :], response_out.at[rows, :], sent.at[0, k]),
            pltpu.make_async_copy(history.at[held, :], history_out.at[held, :], sent.at[1, k]),
        )

    def step(k, carry):
        now, later = lax.rem(k, 2), lax.rem(k + 1, 2)
        fine = jnp.minimum((k + 2) * spacing - 1, steps - 1)
        held = pl.ds(pl.multiple_of(k * cases, cases), cases)
        rows = pl.ds(pl.multiple_of(k * all_ports, all_ports), all_ports)
        for d in range(SLOTS):
            lanes = slice(d * block, (d + 1) * block)
            if carry is None:
                for load in {0: loads[4:5], 1: loads[5:6], 2: loads[6:8], 3: loads[8:]}[d]:
                    load.wait()
            total = times_matrix(operand.at[now], matrices, d)
            diag = miscs[d][DIAG : DIAG + 1, :]
            new = total[:cases] + diag * operand[now, :cases, spot(d)].astype(F32)
            history[held, lanes] = new
            operand[later, :cases, spot(d)] = argument(new, fine, d)
            reply = total[cases:] + diag * state[:, lanes]
            state[:, lanes] = reply
            response[rows, lanes] = reply.astype(BF16)
            operand[later, cases:, spot(d)] = reply.astype(BF16)
        for copy in send(k):
            copy.start()
        return carry

    step(jnp.int32(0), None)
    lax.fori_loop(1, count, step, 0)

    def clear(p, carry):
        rows = pl.ds(pl.multiple_of(p * all_ports, all_ports), all_ports)
        response[rows, :] = jnp.zeros((all_ports, nodes), BF16)
        held = pl.ds(pl.multiple_of(p * cases, cases), cases)
        history[held, :] = jnp.zeros((cases, nodes), F32)
        for copy in send(p):
            copy.start()
        return carry

    lax.fori_loop(count, steps, clear, 0)
    pick = jnp.where(port_columns(all_ports, nodes), 1.0, 0.0).astype(BF16)
    coarse = jnp.dot(history[...].astype(BF16), pick, preferred_element_type=F32)
    forced[: steps * cases, :all_ports] = coarse.astype(BF16)
    pieces = []
    for g in range(steps):
        at = lax.div(jnp.int32(g), spacing) * cases
        rows = pl.ds(pl.multiple_of(at, cases), cases)
        pieces.append(forced[rows, :all_ports].astype(F32))
    wave = jnp.transpose(jnp.concatenate(pieces, axis=0))
    for d in range(SLOTS):
        out[d] = wave[d * ports : (d + 1) * ports].astype(BF16)
    for p in range(steps):
        for copy in send(p):
            copy.wait()


def ports_kernel(meta, response_in, history_in, at_ports, samples, last, response, history,
                 arrived):
    nodes = history.shape[1]
    all_ports = at_ports.shape[1]
    steps = response.shape[0] // all_ports
    cases = history.shape[0] // steps
    first = pltpu.make_async_copy(history_in.at[: steps * cases, :], history, arrived.at[0])
    second = pltpu.make_async_copy(
        response_in.at[: steps * all_ports, :], response, arrived.at[1]
    )
    first.start()
    second.start()
    pick = jnp.where(port_columns(all_ports, nodes), 1.0, 0.0).astype(BF16)
    first.wait()
    high = history[...].astype(BF16)
    low = (history[...] - high.astype(F32)).astype(BF16)
    samples[...] = jnp.dot(high, pick, preferred_element_type=F32)
    samples[...] += jnp.dot(low, pick, preferred_element_type=F32)
    second.wait()
    at_ports[...] = jnp.dot(response[...], pick, preferred_element_type=F32).astype(BF16)
    last[...] = history[pl.ds(pl.multiple_of((meta[0] - 1) * cases, cases), cases), :]


def correct_kernel(meta, response_in, at_ports, last, v0, v1, v2, v3, out, toeplitz,
                   response, arrived):
    cases, nodes = last.shape
    ports, fine_cases = v0.shape
    steps = fine_cases // cases
    block = nodes // SLOTS
    all_ports = SLOTS * ports
    count, spacing = meta[0], meta[1]
    pieces = 4
    part = response.shape[0] // pieces
    copies = []
    for i in range(pieces):
        rows = pl.ds(i * part, part)
        copies.append(
            pltpu.make_async_copy(response_in.at[rows, :], response.at[rows, :], arrived.at[i])
        )
        copies[-1].start()
    drive = jnp.concatenate([v[...] for v in (v0, v1, v2, v3)], axis=0).astype(F32)
    samples_at = jnp.transpose(drive).astype(BF16)
    scratch = toeplitz.at[pl.ds(steps * cases, fine_cases), pl.ds(0, all_ports)]
    scratch[...] = samples_at
    zero = jnp.zeros((cases, all_ports), BF16)
    for i in range(steps):
        fine = jnp.minimum((i + 1) * spacing - 1, steps - 1)
        driven = scratch[pl.ds(pl.multiple_of(fine * cases, cases), cases), :]
        for k in range(i, steps):
            lag = k - i
            toeplitz[k * cases : (k + 1) * cases, lag * all_ports : (lag + 1) * all_ports] = driven
        for lag in range(i + 1, steps):
            toeplitz[i * cases : (i + 1) * cases, lag * all_ports : (lag + 1) * all_ports] = zero
    moved = jnp.dot(toeplitz[: steps * cases, :], at_ports[...], preferred_element_type=F32)
    toe_rows = pl.ds(pl.multiple_of((count - 1) * cases, cases), cases)
    total = last[...]
    for i, copy in enumerate(copies):
        copy.wait()
        rows = slice(i * part, (i + 1) * part)
        total += jnp.dot(toeplitz[toe_rows, rows], response[rows, :], preferred_element_type=F32)
    for d in range(SLOTS):
        out[d, :cases, :] = total[:, d * block : (d + 1) * block]
    return moved


def correct_whole(meta, response, at_ports, samples, last, v0, v1, v2, v3, out, toeplitz, held,
                  response_in, arrived):
    cases = last.shape[0]
    ports, fine_cases = v0.shape
    held[...] = samples[...] + correct_kernel(
        meta, response, at_ports, last, v0, v1, v2, v3, out, toeplitz, response_in, arrived
    )
    pieces = []
    for g in range(fine_cases // cases):
        at = lax.div(jnp.int32(g), meta[1]) * cases
        pieces.append(held[pl.ds(pl.multiple_of(at, cases), cases), :])
    wave = jnp.transpose(jnp.concatenate(pieces, axis=0))
    for d in range(SLOTS):
        out[d, cases:, :] = wave[d * ports : (d + 1) * ports]


def call(kernel, outs, scratch, flops, limit, meta, *operands, hbm_outs=(), hbm_ins=()):
    vmem, hbm = pl.BlockSpec(memory_space=pltpu.VMEM), pl.BlockSpec(memory_space=pltpu.HBM)
    outs = tuple(outs)
    return pl.pallas_call(
        kernel,
        out_shape=outs,
        in_specs=[pl.BlockSpec(memory_space=pltpu.SMEM)]
        + [hbm if i in hbm_ins else vmem for i in range(len(operands))],
        out_specs=tuple(hbm if i in hbm_outs else vmem for i in range(len(outs))),
        scratch_shapes=scratch,
        cost_estimate=pl.CostEstimate(flops=flops, bytes_accessed=12 << 20, transcendentals=0),
        compiler_params=pltpu.CompilerParams(vmem_limit_bytes=limit << 20),
    )(meta, *operands)


def fetch(waves, selector):
    copies = jnp.broadcast_to(waves, (lax.axis_size("sub"), *waves.shape))
    everyone = lax.all_to_all(copies, "sub", split_axis=0, concat_axis=0, tiled=True)
    return jnp.einsum("jr,rjc->jc", selector, everyone, preferred_element_type=F32)


def shards(initial_state, source, inverse_diag, inverse_off, coupling, initial_waves,
           bucket, partner, position_of):
    state, source, matrix = initial_state[0], source[0], inverse_off[0]
    steps, cases, block = source.shape
    nodes = matrix.shape[0]
    subs_all = position_of.shape[0]
    ports = coupling.shape[1]
    all_ports = SLOTS * ports
    x = lax.axis_index("blk")
    rel = lax.rem(x + 4 - 2 * lax.rem(lax.axis_index("sub"), 2), 4)

    count = jnp.where(bucket == 0, steps // 4, jnp.where(bucket == 1, steps // 2, steps))
    spacing = steps // count
    meta = jnp.concatenate([count, spacing, x[None]]).astype(jnp.int32)

    matrices = gather_matrix(matrix)
    injects = jnp.pad(coupling[0][:, None], ((0, 0), (0, block // ports - 1))).reshape(1, block)
    misc = jnp.concatenate([state, inverse_diag, injects, jnp.zeros((6, block), F32)], axis=0)
    miscs = to_home(misc)
    sources = to_home(source)

    identities = jnp.arange(subs_all, dtype=jnp.int32)
    located = jnp.sum(
        jnp.where(partner[0][:, None] == identities[None, :], position_of[None, :], 0), axis=1
    )
    selector = (located[:, None] == identities[None, :]).astype(BF16)

    before = fetch(initial_waves[0], selector)
    incoming = to_home(before.astype(BF16))

    shape = jax.ShapeDtypeStruct
    slots, response, history = call(
        sweep_kernel,
        (shape((SLOTS, ports, steps * cases), BF16), shape((WIDE * steps * all_ports, nodes), BF16),
         shape((WIDE * steps * cases, nodes), F32)),
        [pltpu.VMEM((2, cases + all_ports, nodes), BF16), pltpu.VMEM((all_ports, nodes), F32),
         pltpu.VMEM((steps * cases, nodes), BF16), pltpu.VMEM((steps * all_ports, nodes), BF16),
         pltpu.VMEM((steps * cases, nodes), F32), pltpu.SemaphoreType.DMA((2, steps)),
         *(pltpu.VMEM(m.shape, BF16) for m in matrices), *(pltpu.VMEM(a.shape, BF16) for a in sources),
         pltpu.SemaphoreType.DMA((9,))],
        2 * steps * (cases + all_ports) * nodes * nodes, LIMITS[0], meta,
        *matrices, *sources, *miscs, *incoming, hbm_outs=(1, 2), hbm_ins=range(9),
    )
    at_ports, samples, last = call(
        ports_kernel,
        (shape((steps * all_ports, all_ports), BF16), shape((steps * cases, all_ports), F32),
         shape((cases, nodes), F32)),
        [pltpu.VMEM((steps * all_ports, nodes), BF16), pltpu.VMEM((steps * cases, nodes), F32),
         pltpu.SemaphoreType.DMA((2,))],
        2 * steps * (all_ports + 2 * cases) * nodes * all_ports, LIMITS[1], meta,
        response, history, hbm_ins=(0, 1),
    )

    waves = from_home(slots, rel)
    after = fetch(waves, selector)
    gain = spacing.astype(F32) * coupling[0]
    drives = turn((gain[:, None] * (after - before)).astype(BF16))
    (result,) = call(
        correct_whole,
        (shape((SLOTS, cases + ports, block), F32),),
        [pltpu.VMEM((2 * steps * cases, steps * all_ports), BF16),
         pltpu.VMEM((steps * cases, all_ports), F32),
         pltpu.VMEM((steps * all_ports, nodes), BF16), pltpu.SemaphoreType.DMA((4,))],
        2 * cases * steps * all_ports * nodes, LIMITS[2], meta,
        response, at_ports, samples, last, *drives, hbm_ins=(0,),
    )
    result = from_home(result, rel)
    return result[None, :cases], result[None, cases:]


LIMITS = (45, 45, 45)


def solution(mesh):
    return jax.shard_map(
        shards,
        mesh=mesh,
        in_specs=(
            P("sub", None, "blk"),
            P("sub", None, None, "blk"),
            P("sub", "blk"),
            P("sub", None, "blk"),
            P("sub", "blk"),
            P("sub", "blk", None),
            P("sub"),
            P("sub", "blk"),
            P(),
        ),
        out_specs=(P("sub", None, "blk"), P("sub", "blk", None)),
        check_vma=False,
    )
```

profile of v0, /device:TPU:0, one launch (start us, length us, event | category | flops | bytes accessed | tf_op | source)
XLA Modules:
  0.0 186.0 jit_solution(6944269878461408444)
XLA Ops:
  0.7 2.6 %slice_bitcast_fusion = bf16[1280,512]{1,0:T(8,128)(2,1)} fusion(bf16[1,2048,512]{2,1,0:T(8,128)(2,1)} %param.12), kind=kLoop, calls=%fused_computation | loop fusion | bytes 2621440 | tf_op jit(solution)/shard_map/slice | solution.py:46
  3.3 1.8 collective-permute-start.1
  6.4 1.3 collective-permute-start.5
  8.0 1.3 collective-permute-start.9
  9.3 1.3 collective-permute-start.10
  10.6 23.9 %collective-permute-done.9.m1 = f32[72,512]{1,0:T(8,128)S(1)} collective-permute-done((f32[72,512]{1,0:T(8,128)S(1)}, f32[72,512]{1,0:T(8,128)S(1)}, u32[]{:S(2)}, u32[]{:S(2)}) %collective-permute-start.9) | collective-permute-done | bytes 147488 | tf_op jit(solution)/shard_map/ppermute | solution.py:21
  35.9 1.3 collective-permute-start.6
  38.1 4.7 %collective-permute-done.11.m3 = f32[72,512]{1,0:T(8,128)S(1)} collective-permute-done((f32[72,512]{1,0:T(8,128)S(1)}, f32[72,512]{1,0:T(8,128)S(1)}, u32[]{:S(2)}, u32[]{:S(2)}) %collective-permute-start.11) | collective-permute-done | bytes 147488 | tf_op jit(solution)/shard_map/ppermute | solution.py:21
  42.8 1.6 collective-permute-start.3
  45.5 8.6 %all-to-all-start = ((bf16[32,32,512]{2,1,0:T(8,128)(2,1)}), bf16[32,32,512]{2,1,0:T(8,128)(2,1)}, u32[]{:S(2)}, u32[]{:S(2)}) async-start(bf16[32,32,512]{2,1,0:T(8,128)(2,1)} %broadcast_in_dim.45), calls=%async_computation | async-start | bytes 2097152 | tf_op jit(solution)/shard_map/all_to_all | solution.py:275
  54.1 1.3 collective-permute-start.2
  57.5 1.3 collective-permute-start.4
  58.8 10.3 %collective-permute-done.7.s2_in = bf16[8,64,512]{2,1,0:T(8,128)(2,1)S(1)} collective-permute-done((bf16[8,64,512]{2,1,0:T(8,128)(2,1)}, bf16[8,64,512]{2,1,0:T(8,128)(2,1)S(1)}, u32[]{:S(2)}, u32[]{:S(2)}) %collective-permute-start.7) | collective-permute-done | bytes 524320 | tf_op jit(solution)/shard_map/ppermute | solution.py:21
  71.4 1.9 %fusion.2 = f32[32,1,512]{2,1,0:T(1,128)S(1)} fusion(bf16[32,32,512]{2,1,0:T(8,128)(2,1)} %all-to-all-done, pred[32,32,1]{1,0,2:T(32,128)(4,1)S(1)} %fusion.9), kind=kOutput, calls=%fused_computation.3 | convolution fusion | flops 1048576 | bytes 1115136 | tf_op jit(solution)/shard_map/jr,rjc->jc/dot_general | solution.py:276
  73.4 9.7 %collective-permute-done.8.s3_in = bf16[8,64,512]{2,1,0:T(8,128)(2,1)} collective-permute-done((bf16[8,64,512]{2,1,0:T(8,128)(2,1)}, bf16[8,64,512]{2,1,0:T(8,128)(2,1)}, u32[]{:S(2)}, u32[]{:S(2)}) %collective-permute-start.8) | collective-permute-done | bytes 524320 | tf_op jit(solution)/shard_map/ppermute | solution.py:21
  84.4 4.5 %collective-permute-done.12.w1 = bf16[32,512]{1,0:T(8,128)(2,1)S(1)} collective-permute-done((bf16[32,512]{1,0:T(8,128)(2,1)S(1)}, bf16[32,512]{1,0:T(8,128)(2,1)S(1)}, u32[]{:S(2)}, u32[]{:S(2)}) %collective-permute-start.12) | collective-permute-done | bytes 32800 | tf_op jit(solution)/shard_map/ppermute | solution.py:21
  90.9 5.3 %collective-permute-done.13.w2 = bf16[32,512]{1,0:T(8,128)(2,1)S(1)} collective-permute-done((bf16[32,512]{1,0:T(8,128)(2,1)S(1)}, bf16[32,512]{1,0:T(8,128)(2,1)S(1)}, u32[]{:S(2)}, u32[]{:S(2)}) %collective-permute-start.13) | collective-permute-done | bytes 32800 | tf_op jit(solution)/shard_map/ppermute | solution.py:21
  98.2 5.6 %collective-permute-done.14.w3 = bf16[32,512]{1,0:T(8,128)(2,1)S(1)} collective-permute-done((bf16[32,512]{1,0:T(8,128)(2,1)S(1)}, bf16[32,512]{1,0:T(8,128)(2,1)S(1)}, u32[]{:S(2)}, u32[]{:S(2)}) %collective-permute-start.14) | collective-permute-done | bytes 32800 | tf_op jit(solution)/shard_map/ppermute | solution.py:21
  107.6 21.4 %shard_map.104 = (bf16[4,32,512]{2,1,0:T(8,128)(2,1)S(1)}, bf16[5120,2048]{1,0:T(8,128)(2,1)}, f32[2560,2048]{1,0:T(8,128)}) custom-call(s32[3]{0:T(128)S(1)} %pad_add_fusion.meta, bf16[2048,512]{1,0:T(8,128)(2,1)S(1)} %bitcast.50, bf16[2048,512]{1,0:T(8,128)(2,1)} %collective-permute-done.a1_in, bf16[1280,512]{1,0:T(8,128)(2,1)} %collective-permute-done.2.a2_in, ...), custom_call_target="tpu_custom_call" | custom-call | flops 12884901888 | bytes 12582912 | tf_op jit(solution)/shard_map/pallas_call | solution.py:261
  129.0 1.3 collective-permute-start.15
  130.3 1.3 collective-permute-start.16
  131.6 1.3 collective-permute-start.17
  133.2 1.3 collective-permute-done.17
  135.7 5.5 %all-to-all-start.1 = ((bf16[32,32,512]{2,1,0:T(8,128)(2,1)}), bf16[32,32,512]{2,1,0:T(8,128)(2,1)S(1)}, u32[]{:S(2)}, u32[]{:S(2)}) async-start(bf16[32,32,512]{2,1,0:T(8,128)(2,1)} %broadcast_in_dim.46), calls=%async_computation.1 | async-start | bytes 2097152 | tf_op jit(solution)/shard_map/all_to_all | solution.py:275
  141.2 17.2 %all-to-all-done.1 = bf16[32,32,512]{2,1,0:T(8,128)(2,1)S(1)} async-done(((bf16[32,32,512]{2,1,0:T(8,128)(2,1)}), bf16[32,32,512]{2,1,0:T(8,128)(2,1)S(1)}, u32[]{:S(2)}, u32[]{:S(2)}) %all-to-all-start.1) | async-done | bytes 1048608 | tf_op jit(solution)/shard_map/all_to_all | solution.py:275
  159.2 3.5 %collective-permute-start.18 = (bf16[32,512]{1,0:T(8,128)(2,1)S(1)}, bf16[32,512]{1,0:T(8,128)(2,1)S(1)}, u32[]{:S(2)}, u32[]{:S(2)}) collective-permute-start(bf16[32,512]{1,0:T(8,128)(2,1)S(1)} %fusion.6.v0), channel_id=1, source_target_pairs={{1,0},{2,1},{3,2},{0,3},{5,4},{6,5},{7,6},{4,7},{9,8},{10,9},{11,1... | collective-permute-start | bytes 98312 | tf_op jit(solution)/shard_map/ppermute | solution.py:32
  163.7 7.4 %shard_map.105 = (bf16[1024,128]{1,0:T(8,128)(2,1)S(1)}, f32[512,128]{1,0:T(8,128)S(1)}, f32[64,2048]{1,0:T(8,128)S(1)}) custom-call(s32[3]{0:T(128)S(1)} %pad_add_fusion.meta, bf16[5120,2048]{1,0:T(8,128)(2,1)} %get-tuple-element.8.response_in.response, f32[2560,2048]{1,0:T(8,128)} %get-tuple-element.9.history_in), custom_call_target="tpu_custom_call" | custom-call | flops 1073741824 | bytes 12582912 | tf_op jit(solution)/shard_map/pallas_call | solution.py:261
  171.1 3.2 %shard_map.106 = f32[4,96,512]{2,1,0:T(8,128)S(1)} custom-call(s32[3]{0:T(128)S(1)} %pad_add_fusion.meta, bf16[5120,2048]{1,0:T(8,128)(2,1)} %get-tuple-element.8.response_in.response, bf16[1024,128]{1,0:T(8,128)(2,1)S(1)} %get-tuple-element.10.at_ports, f32[512,128]{1,0:T(8,128)S(1)} %get-tuple-element.11.samples, f32[64,2048]{1,0:T(8,128)S(1)} %get-tuple-element.12.last, ...), custom_call_target="tpu_custom_call" | custom-call | flops 268435456 | bytes 12582912 | tf_op jit(solution)/shard_map/pallas_call | solution.py:261
  174.4 4.5 %collective-permute-start.21 = (f32[96,512]{1,0:T(8,128)S(1)}, f32[96,512]{1,0:T(8,128)S(1)}, u32[]{:S(2)}, u32[]{:S(2)}) collective-permute-start(f32[96,512]{1,0:T(8,128)S(1)} %get-tuple-element.16), channel_id=1, source_target_pairs={{0,1},{6,7},{8,9},{14,15},{16,17},{22,23},{24,25},{30,31},{32,33},... | collective-permute-start | bytes 589832 | tf_op jit(solution)/shard_map/ppermute | solution.py:21
  178.8 1.3 collective-permute-start.22
  180.1 1.3 collective-permute-start.23
  182.0 2.1 %collective-permute-done.22 = f32[96,512]{1,0:T(8,128)S(1)} collective-permute-done((f32[96,512]{1,0:T(8,128)S(1)}, f32[96,512]{1,0:T(8,128)S(1)}, u32[]{:S(2)}, u32[]{:S(2)}) %collective-permute-start.22) | collective-permute-done | bytes 196640 | tf_op jit(solution)/shard_map/ppermute | solution.py:21
  (81 shorter events, 23.3 us)
Async XLA Ops:
  0.7 43.7 %copy-start.12 = (bf16[1,32,512]{2,1,0:T(8,128)(2,1)S(1)}, bf16[1,32,512]{2,1,0:T(8,128)(2,1)}, u32[]{:S(2)}) copy-start(bf16[1,32,512]{2,1,0:T(8,128)(2,1)} %param.14) | copy-start | bytes 98308
  3.3 50.8 %collective-permute-start.1 = (bf16[1280,512]{1,0:T(8,128)(2,1)}, bf16[1280,512]{1,0:T(8,128)(2,1)}, u32[]{:S(2)}, u32[]{:S(2)}) collective-permute-start(bf16[1280,512]{1,0:T(8,128)(2,1)} %slice_bitcast_fusion), channel_id=1, source_target_pairs={{2,1},{4,7},{10,9},{12,15},{18,17},{20,23},{26,25},{28,31},{34,33}... | collective-permute-start | bytes 3932168 | tf_op jit(solution)/shard_map/ppermute | solution.py:21
  5.1 98.8 %collective-permute-start = (bf16[2048,512]{1,0:T(8,128)(2,1)S(1)}, bf16[2048,512]{1,0:T(8,128)(2,1)}, u32[]{:S(2)}, u32[]{:S(2)}) collective-permute-start(bf16[2048,512]{1,0:T(8,128)(2,1)S(1)} %bitcast.48), channel_id=1, source_target_pairs={{1,0},{7,6},{9,8},{15,14},{17,16},{23,22},{25,24},{31,30},{33,32},... | collective-permute-start | bytes 6291464 | tf_op jit(solution)/shard_map/ppermute | solution.py:21
  6.4 97.5 %collective-permute-start.5 = (bf16[2048,512]{1,0:T(8,128)(2,1)S(1)}, bf16[2048,512]{1,0:T(8,128)(2,1)}, u32[]{:S(2)}, u32[]{:S(2)}) collective-permute-start(bf16[2048,512]{1,0:T(8,128)(2,1)S(1)} %bitcast.49), channel_id=1, source_target_pairs={{3,0},{5,6},{11,8},{13,14},{19,16},{21,22},{27,24},{29,30},{35,32}... | collective-permute-start | bytes 6291464 | tf_op jit(solution)/shard_map/ppermute | solution.py:21
  8.0 26.5 %collective-permute-start.9 = (f32[72,512]{1,0:T(8,128)S(1)}, f32[72,512]{1,0:T(8,128)S(1)}, u32[]{:S(2)}, u32[]{:S(2)}) collective-permute-start(f32[72,512]{1,0:T(8,128)S(1)} %maximum_maximum_fusion.m0), channel_id=1, source_target_pairs={{1,0},{7,6},{9,8},{15,14},{17,16},{23,22},{25,24},{31,30},{33,32},... | collective-permute-start | bytes 442376 | tf_op jit(solution)/shard_map/ppermute | solution.py:21
  9.3 26.5 %collective-permute-start.10 = (f32[72,512]{1,0:T(8,128)S(1)}, f32[72,512]{1,0:T(8,128)S(1)}, u32[]{:S(2)}, u32[]{:S(2)}) collective-permute-start(f32[72,512]{1,0:T(8,128)S(1)} %maximum_maximum_fusion.m0), channel_id=1, source_target_pairs={{2,0},{4,6},{10,8},{12,14},{18,16},{20,22},{26,24},{28,30},{34,32}... | collective-permute-start | bytes 442376 | tf_op jit(solution)/shard_map/ppermute | solution.py:21
  34.6 8.2 %collective-permute-start.11 = (f32[72,512]{1,0:T(8,128)S(1)}, f32[72,512]{1,0:T(8,128)S(1)}, u32[]{:S(2)}, u32[]{:S(2)}) collective-permute-start(f32[72,512]{1,0:T(8,128)S(1)} %maximum_maximum_fusion.m0), channel_id=1, source_target_pairs={{3,0},{5,6},{11,8},{13,14},{19,16},{21,22},{27,24},{29,30},{35,32}... | collective-permute-start | bytes 442376 | tf_op jit(solution)/shard_map/ppermute | solution.py:21
  35.9 35.3 %copy-start.15 = (s32[32]{0:T(128)S(1)}, s32[32]{0:T(128)}, u32[]{:S(2)}) copy-start(s32[32]{0:T(128)} %param.17) | copy-start | bytes 388
  35.9 35.3 %copy-start.16 = (s32[1,32]{1,0:T(1,128)S(1)}, s32[1,32]{1,0:T(1,128)}, u32[]{:S(2)}) copy-start(s32[1,32]{1,0:T(1,128)} %param.16) | copy-start | bytes 388
  35.9 19.5 %collective-permute-start.6 = (bf16[8,64,512]{2,1,0:T(8,128)(2,1)}, bf16[8,64,512]{2,1,0:T(8,128)(2,1)S(1)}, u32[]{:S(2)}, u32[]{:S(2)}) collective-permute-start(bf16[8,64,512]{2,1,0:T(8,128)(2,1)} %bitcast.4.s0_in), channel_id=1, source_target_pairs={{1,0},{7,6},{9,8},{15,14},{17,16},{23,22},{25,24},{31,30},{33,32},... | collective-permute-start | bytes 1572872 | tf_op jit(solution)/shard_map/ppermute | solution.py:21
  42.8 14.7 %copy-start.5 = (f32[72,512]{1,0:T(8,128)}, f32[72,512]{1,0:T(8,128)S(1)}, u32[]{:S(2)}) copy-start(f32[72,512]{1,0:T(8,128)S(1)} %collective-permute-done.11.m3) | copy-start | bytes 442372
  42.8 14.7 %collective-permute-start.3 = (bf16[768,512]{1,0:T(8,128)(2,1)}, bf16[768,512]{1,0:T(8,128)(2,1)}, u32[]{:S(2)}, u32[]{:S(2)}) collective-permute-start(bf16[768,512]{1,0:T(8,128)(2,1)} %slice_bitcast_fusion.1), channel_id=1, source_target_pairs={{2,3},{4,5},{10,11},{12,13},{18,19},{20,21},{26,27},{28,29},{34,35... | collective-permute-start | bytes 2359304 | tf_op jit(solution)/shard_map/ppermute | solution.py:21
  45.5 26.0 %all-to-all-start = ((bf16[32,32,512]{2,1,0:T(8,128)(2,1)}), bf16[32,32,512]{2,1,0:T(8,128)(2,1)}, u32[]{:S(2)}, u32[]{:S(2)}) async-start(bf16[32,32,512]{2,1,0:T(8,128)(2,1)} %broadcast_in_dim.45), calls=%async_computation | async-start | bytes 2097152 | tf_op jit(solution)/shard_map/all_to_all | solution.py:275
  54.1 49.8 %collective-permute-start.2 = (bf16[1280,512]{1,0:T(8,128)(2,1)}, bf16[1280,512]{1,0:T(8,128)(2,1)}, u32[]{:S(2)}, u32[]{:S(2)}) collective-permute-start(bf16[1280,512]{1,0:T(8,128)(2,1)} %collective-permute-done.1), channel_id=1, source_target_pairs={{1,0},{7,6},{9,8},{15,14},{17,16},{23,22},{25,24},{31,30},{33,32},... | collective-permute-start | bytes 3932168 | tf_op jit(solution)/shard_map/ppermute | solution.py:21
  56.2 12.9 %collective-permute-start.7 = (bf16[8,64,512]{2,1,0:T(8,128)(2,1)}, bf16[8,64,512]{2,1,0:T(8,128)(2,1)S(1)}, u32[]{:S(2)}, u32[]{:S(2)}) collective-permute-start(bf16[8,64,512]{2,1,0:T(8,128)(2,1)} %bitcast.4.s0_in), channel_id=1, source_target_pairs={{2,0},{4,6},{10,8},{12,14},{18,16},{20,22},{26,24},{28,30},{34,32}... | collective-permute-start | bytes 1572872 | tf_op jit(solution)/shard_map/ppermute | solution.py:21
  57.5 46.3 %collective-permute-start.4 = (bf16[768,512]{1,0:T(8,128)(2,1)}, bf16[768,512]{1,0:T(8,128)(2,1)S(1)}, u32[]{:S(2)}, u32[]{:S(2)}) collective-permute-start(bf16[768,512]{1,0:T(8,128)(2,1)} %collective-permute-done.3), channel_id=1, source_target_pairs={{3,0},{5,6},{11,8},{13,14},{19,16},{21,22},{27,24},{29,30},{35,32}... | collective-permute-start | bytes 2359304 | tf_op jit(solution)/shard_map/ppermute | solution.py:21
  69.9 13.2 %collective-permute-start.8 = (bf16[8,64,512]{2,1,0:T(8,128)(2,1)}, bf16[8,64,512]{2,1,0:T(8,128)(2,1)}, u32[]{:S(2)}, u32[]{:S(2)}) collective-permute-start(bf16[8,64,512]{2,1,0:T(8,128)(2,1)} %bitcast.4.s0_in), channel_id=1, source_target_pairs={{3,0},{5,6},{11,8},{13,14},{19,16},{21,22},{27,24},{29,30},{35,32}... | collective-permute-start | bytes 1572872 | tf_op jit(solution)/shard_map/ppermute | solution.py:21
  73.4 11.0 %copy-start.9 = (f32[32,1,512]{2,1,0:T(1,128)}, f32[32,1,512]{2,1,0:T(1,128)S(1)}, u32[]{:S(2)}) copy-start(f32[32,1,512]{2,1,0:T(1,128)S(1)} %fusion.2) | copy-start | bytes 196612
  83.1 5.8 %collective-permute-start.12 = (bf16[32,512]{1,0:T(8,128)(2,1)S(1)}, bf16[32,512]{1,0:T(8,128)(2,1)S(1)}, u32[]{:S(2)}, u32[]{:S(2)}) collective-permute-start(bf16[32,512]{1,0:T(8,128)(2,1)S(1)} %bitcast.51), channel_id=1, source_target_pairs={{1,0},{7,6},{9,8},{15,14},{17,16},{23,22},{25,24},{31,30},{33,32},... | collective-permute-start | bytes 98312 | tf_op jit(solution)/shard_map/ppermute | solution.py:21
  88.9 7.3 %collective-permute-start.13 = (bf16[32,512]{1,0:T(8,128)(2,1)S(1)}, bf16[32,512]{1,0:T(8,128)(2,1)S(1)}, u32[]{:S(2)}, u32[]{:S(2)}) collective-permute-start(bf16[32,512]{1,0:T(8,128)(2,1)S(1)} %bitcast.52), channel_id=1, source_target_pairs={{2,0},{4,6},{10,8},{12,14},{18,16},{20,22},{26,24},{28,30},{34,32}... | collective-permute-start | bytes 98312 | tf_op jit(solution)/shard_map/ppermute | solution.py:21
  96.8 7.0 %collective-permute-start.14 = (bf16[32,512]{1,0:T(8,128)(2,1)S(1)}, bf16[32,512]{1,0:T(8,128)(2,1)S(1)}, u32[]{:S(2)}, u32[]{:S(2)}) collective-permute-start(bf16[32,512]{1,0:T(8,128)(2,1)S(1)} %bitcast.53), channel_id=1, source_target_pairs={{3,0},{5,6},{11,8},{13,14},{19,16},{21,22},{27,24},{29,30},{35,32}... | collective-permute-start | bytes 98312 | tf_op jit(solution)/shard_map/ppermute | solution.py:21
  129.0 3.9 %collective-permute-start.15 = (bf16[32,512]{1,0:T(8,128)(2,1)S(1)}, bf16[32,512]{1,0:T(8,128)(2,1)S(1)}, u32[]{:S(2)}, u32[]{:S(2)}) collective-permute-start(bf16[32,512]{1,0:T(8,128)(2,1)S(1)} %get-tuple-element.19), channel_id=1, source_target_pairs={{0,1},{6,7},{8,9},{14,15},{16,17},{22,23},{24,25},{30,31},{32,33},... | collective-permute-start | bytes 98312 | tf_op jit(solution)/shard_map/ppermute | solution.py:21
  130.3 2.9 %collective-permute-start.16 = (bf16[32,512]{1,0:T(8,128)(2,1)S(1)}, bf16[32,512]{1,0:T(8,128)(2,1)S(1)}, u32[]{:S(2)}, u32[]{:S(2)}) collective-permute-start(bf16[32,512]{1,0:T(8,128)(2,1)S(1)} %get-tuple-element.18), channel_id=1, source_target_pairs={{0,2},{6,4},{8,10},{14,12},{16,18},{22,20},{24,26},{30,28},{32,34}... | collective-permute-start | bytes 98312 | tf_op jit(solution)/shard_map/ppermute | solution.py:21
  131.6 2.9 %collective-permute-start.17 = (bf16[32,512]{1,0:T(8,128)(2,1)S(1)}, bf16[32,512]{1,0:T(8,128)(2,1)S(1)}, u32[]{:S(2)}, u32[]{:S(2)}) collective-permute-start(bf16[32,512]{1,0:T(8,128)(2,1)S(1)} %get-tuple-element.17), channel_id=1, source_target_pairs={{0,3},{6,5},{8,11},{14,13},{16,19},{22,21},{24,27},{30,29},{32,35}... | collective-permute-start | bytes 98312 | tf_op jit(solution)/shard_map/ppermute | solution.py:21
  134.5 24.6 %copy-start.10 = (f32[32,1,512]{2,1,0:T(1,128)S(1)}, f32[32,1,512]{2,1,0:T(1,128)}, u32[]{:S(2)}) copy-start(f32[32,1,512]{2,1,0:T(1,128)} %copy-done.9) | copy-start | bytes 196612
  135.7 22.8 %all-to-all-start.1 = ((bf16[32,32,512]{2,1,0:T(8,128)(2,1)}), bf16[32,32,512]{2,1,0:T(8,128)(2,1)S(1)}, u32[]{:S(2)}, u32[]{:S(2)}) async-start(bf16[32,32,512]{2,1,0:T(8,128)(2,1)} %broadcast_in_dim.46), calls=%async_computation.1 | async-start | bytes 2097152 | tf_op jit(solution)/shard_map/all_to_all | solution.py:275
  159.2 11.9 %collective-permute-start.18 = (bf16[32,512]{1,0:T(8,128)(2,1)S(1)}, bf16[32,512]{1,0:T(8,128)(2,1)S(1)}, u32[]{:S(2)}, u32[]{:S(2)}) collective-permute-start(bf16[32,512]{1,0:T(8,128)(2,1)S(1)} %fusion.6.v0), channel_id=1, source_target_pairs={{1,0},{2,1},{3,2},{0,3},{5,4},{6,5},{7,6},{4,7},{9,8},{10,9},{11,1... | collective-permute-start | bytes 98312 | tf_op jit(solution)/shard_map/ppermute | solution.py:32
  162.7 8.3 %collective-permute-start.19 = (bf16[32,512]{1,0:T(8,128)(2,1)S(1)}, bf16[32,512]{1,0:T(8,128)(2,1)S(1)}, u32[]{:S(2)}, u32[]{:S(2)}) collective-permute-start(bf16[32,512]{1,0:T(8,128)(2,1)S(1)} %fusion.6.v0), channel_id=1, source_target_pairs={{2,0},{3,1},{0,2},{1,3},{6,4},{7,5},{4,6},{5,7},{10,8},{11,9},{8,1... | collective-permute-start | bytes 98312 | tf_op jit(solution)/shard_map/ppermute | solution.py:32
  162.7 8.3 %collective-permute-start.20 = (bf16[32,512]{1,0:T(8,128)(2,1)S(1)}, bf16[32,512]{1,0:T(8,128)(2,1)S(1)}, u32[]{:S(2)}, u32[]{:S(2)}) collective-permute-start(bf16[32,512]{1,0:T(8,128)(2,1)S(1)} %fusion.6.v0), channel_id=1, source_target_pairs={{3,0},{0,1},{1,2},{2,3},{7,4},{4,5},{5,6},{6,7},{11,8},{8,9},{9,10... | collective-permute-start | bytes 98312 | tf_op jit(solution)/shard_map/ppermute | solution.py:32
  174.4 7.6 %collective-permute-start.21 = (f32[96,512]{1,0:T(8,128)S(1)}, f32[96,512]{1,0:T(8,128)S(1)}, u32[]{:S(2)}, u32[]{:S(2)}) collective-permute-start(f32[96,512]{1,0:T(8,128)S(1)} %get-tuple-element.16), channel_id=1, source_target_pairs={{0,1},{6,7},{8,9},{14,15},{16,17},{22,23},{24,25},{30,31},{32,33},... | collective-permute-start | bytes 589832 | tf_op jit(solution)/shard_map/ppermute | solution.py:21
  178.8 5.3 %collective-permute-start.22 = (f32[96,512]{1,0:T(8,128)S(1)}, f32[96,512]{1,0:T(8,128)S(1)}, u32[]{:S(2)}, u32[]{:S(2)}) collective-permute-start(f32[96,512]{1,0:T(8,128)S(1)} %get-tuple-element.15), channel_id=1, source_target_pairs={{0,2},{6,4},{8,10},{14,12},{16,18},{22,20},{24,26},{30,28},{32,34}... | collective-permute-start | bytes 589832 | tf_op jit(solution)/shard_map/ppermute | solution.py:21
  180.1 4.5 %collective-permute-start.23 = (f32[96,512]{1,0:T(8,128)S(1)}, f32[96,512]{1,0:T(8,128)S(1)}, u32[]{:S(2)}, u32[]{:S(2)}) collective-permute-start(f32[96,512]{1,0:T(8,128)S(1)} %get-tuple-element.14), channel_id=1, source_target_pairs={{0,3},{6,5},{8,11},{14,13},{16,19},{22,21},{24,27},{30,29},{32,35}... | collective-permute-start | bytes 589832 | tf_op jit(solution)/shard_map/ppermute | solution.py:21
  (11 other events, 32.0 us)
where the time goes:
time: 188 us; the launch traced here: 186 us
  waiting for transfers between devices  86 us (46%)
  starting transfers between devices  49.6 us (26%)
  Pallas kernels  32 us (17%)
  local copies, waits for them, and re-layouts  13.4 us (7%)
  matrix products  2.62 us (1%)
    ppermute x21, waiting for transfers between devices, hop(): return lax.ppermute(array, ('sub', 'blk'), pairs)  68.8 us
    pallas_call x3, Pallas kernels, call(): pl.pallas_call(kernel, out_shape=outs, in_specs=[pl.BlockSpec(memory_spac...  32 us
    ppermute x21, starting transfers between devices, hop(): return lax.ppermute(array, ('sub', 'blk'), pairs)  31 us
    all_to_all x2, waiting for transfers between devices, fetch(): lax.all_to_all(copies, 'sub', split_axis=0, concat_axis=0, tiled=True)  17.2 us
    all_to_all x2, starting transfers between devices, fetch(): lax.all_to_all(copies, 'sub', split_axis=0, concat_axis=0, tiled=True)  14.1 us
    unnamed x35, local copies, waits for them, and re-layouts  6.09 us
    ppermute x3, starting transfers between devices, turn(): parts.append(lax.ppermute(array, ('sub', 'blk'), pairs))  4.49 us
  transfers between devices with their start and end apart: 26, of which 13 were waited for; matrix products, arithmetic and copies ran while one was open for 2% of the time, Pallas kernels for 4%

commit v1 on v0

--- a/solution.py
+++ b/solution.py
@@ -33,11 +33,13 @@
     return tuple(parts)
 
 
-def from_home(slots, rel):
-    one, two, three = (hop(slots[d], 0, d) for d in (1, 2, 3))
-    return jnp.where(
-        rel == 0, slots[0], jnp.where(rel == 1, one, jnp.where(rel == 2, two, three))
-    )
+def from_home(slots):
+    return slots[0], *(hop(slots[d], 0, d) for d in (1, 2, 3))
+
+
+def mine(parts, rel, rows=slice(None)):
+    zero, one, two, three = (part[rows] for part in parts)
+    return jnp.where(rel == 0, zero, jnp.where(rel == 1, one, jnp.where(rel == 2, two, three)))
 
 
 def gather_matrix(matrix):
@@ -270,10 +272,42 @@
     )(meta, *operands)
 
 
-def fetch(waves, selector):
-    copies = jnp.broadcast_to(waves, (lax.axis_size("sub"), *waves.shape))
+def first_fetch(waves, partner, position_of):
+    subs = lax.axis_size("sub")
+    ports = waves.shape[0]
+    ids = jnp.pad(partner.astype(BF16)[None, :], ((0, 15), (0, waves.shape[1] - ports)))
+    copies = jnp.broadcast_to(jnp.concatenate([waves, ids], axis=0), (subs, ports + 16, waves.shape[1]))
     everyone = lax.all_to_all(copies, "sub", split_axis=0, concat_axis=0, tiled=True)
-    return jnp.einsum("jr,rjc->jc", selector, everyone, preferred_element_type=F32)
+    identities = jnp.arange(subs, dtype=jnp.int32)
+
+    def locate(ids):
+        return jnp.sum(
+            jnp.where(ids[..., None] == identities, position_of, 0), axis=-1, dtype=jnp.int32
+        )
+
+    selector = (locate(partner)[:, None] == identities[None, :]).astype(BF16)
+    incoming = jnp.einsum(
+        "jr,rjc->jc", selector, everyone[:, :ports], preferred_element_type=F32
+    )
+    return incoming, locate(everyone[:, ports, :ports].astype(jnp.int32))
+
+
+def second_fetch(waves, located):
+    subs = lax.axis_size("sub")
+    sub = lax.axis_index("sub")
+    swap = [(s * SLOTS + r, (s ^ 1) * SLOTS + r) for s in range(subs) for r in range(SLOTS)]
+    others = lax.ppermute(waves, ("sub", "blk"), swap)
+    pairs = located.reshape(subs // 2, 2, -1)
+    wanted = jnp.where(lax.rem(sub, 2) == 0, pairs[:, 0], pairs[:, 1])[:, :, None]
+    zero = jnp.zeros((), BF16)
+    sent = jnp.where(
+        wanted == sub, waves[None], jnp.where(wanted == (sub ^ 1), others[None], zero)
+    )
+    groups = [[s for s in range(subs) if s % 2 == core] for core in (0, 1)]
+    parts = lax.all_to_all(
+        sent, "sub", split_axis=0, concat_axis=0, axis_index_groups=groups, tiled=True
+    )
+    return jnp.sum(parts.astype(F32), axis=0)
 
 
 def shards(initial_state, source, inverse_diag, inverse_off, coupling, initial_waves,
@@ -281,7 +315,6 @@
     state, source, matrix = initial_state[0], source[0], inverse_off[0]
     steps, cases, block = source.shape
     nodes = matrix.shape[0]
-    subs_all = position_of.shape[0]
     ports = coupling.shape[1]
     all_ports = SLOTS * ports
     x = lax.axis_index("blk")
@@ -297,13 +330,7 @@
     miscs = to_home(misc)
     sources = to_home(source)
 
-    identities = jnp.arange(subs_all, dtype=jnp.int32)
-    located = jnp.sum(
-        jnp.where(partner[0][:, None] == identities[None, :], position_of[None, :], 0), axis=1
-    )
-    selector = (located[:, None] == identities[None, :]).astype(BF16)
-
-    before = fetch(initial_waves[0], selector)
+    before, located = first_fetch(initial_waves[0], partner[0], position_of)
     incoming = to_home(before.astype(BF16))
 
     shape = jax.ShapeDtypeStruct
@@ -329,8 +356,8 @@
         response, history, hbm_ins=(0, 1),
     )
 
-    waves = from_home(slots, rel)
-    after = fetch(waves, selector)
+    waves = mine(from_home(slots), rel)
+    after = second_fetch(waves, located)
     gain = spacing.astype(F32) * coupling[0]
     drives = turn((gain[:, None] * (after - before)).astype(BF16))
     (result,) = call(
@@ -342,8 +369,10 @@
         2 * cases * steps * all_ports * nodes, LIMITS[2], meta,
         response, at_ports, samples, last, *drives, hbm_ins=(0,),
     )
-    result = from_home(result, rel)
-    return result[None, :cases], result[None, cases:]
+    parts = from_home(result)
+    last = mine(parts, rel, slice(0, cases))
+    waveform = mine(parts, rel, slice(cases, None))
+    return last[None], waveform[None]
 
 
 LIMITS = (45, 45, 45)

time: 188 us -> 180 us (0.957)
  waiting for transfers between devices: 86 us -> 80 us
  local copies, waits for them, and re-layouts: 13.4 us -> 7.82 us
  other arithmetic: 0.56 us -> 4.62 us
  matrix products: 2.62 us -> 0.7 us
  starting transfers between devices: 49.6 us -> 51.5 us
    all_to_all x2, waiting for transfers between devices: 17.2 us -> 11.8 us  [the longest x1 11.8 us: second_fetch(): lax.all_to_all(sent, 'sub', split_axis=0, concat_axis=0, axis_index_group...]
    unnamed x35 -> x26, local copies, waits for them, and re-layouts: 6.09 us -> 1.47 us
    all_to_all x2, starting transfers between devices: 14.1 us -> 17.3 us  [the longest x1 12 us: first_fetch(): lax.all_to_all(copies, 'sub', split_axis=0, concat_axis=0, tiled=True)]
    broadcast_in_dim x4 -> x1, local copies, waits for them, and re-layouts: 3.51 us -> 1.33 us  [first_fetch(): jnp.broadcast_to(jnp.concatenate([waves, ids], axis=0), (subs, ports + 16...]
    ppermute x21, starting transfers between devices: 31 us -> 29 us  [hop(): return lax.ppermute(array, ('sub', 'blk'), pairs)]
    dot_general x2 -> x1, matrix products: 2.62 us -> 0.7 us  [first_fetch(): jnp.einsum('jr,rjc->jc', selector, everyone[:, :ports], preferred_element...]
  transfers between devices with their start and end apart: 26 -> 27, of which waited for: 13 -> 14; matrix products, arithmetic and copies ran while one was open for 2% -> 4% of each run, Pallas kernels for 4% -> 4%
where the time goes in v1:
time: 180 us; the launch traced here: 178 us
  waiting for transfers between devices  80 us (44%)
  starting transfers between devices  51.5 us (29%)
  Pallas kernels  32 us (18%)
  local copies, waits for them, and re-layouts  7.82 us (4%)
  other arithmetic  4.62 us (3%)
    ppermute x21, waiting for transfers between devices, hop(): return lax.ppermute(array, ('sub', 'blk'), pairs)  67 us
    pallas_call x3, Pallas kernels, call(): pl.pallas_call(kernel, out_shape=outs, in_specs=[pl.BlockSpec(memory_spac...  32 us
    ppermute x21, starting transfers between devices, hop(): return lax.ppermute(array, ('sub', 'blk'), pairs)  29 us
    all_to_all x1, starting transfers between devices, first_fetch(): lax.all_to_all(copies, 'sub', split_axis=0, concat_axis=0, tiled=True)  12 us
    all_to_all x1, waiting for transfers between devices, second_fetch(): lax.all_to_all(sent, 'sub', split_axis=0, concat_axis=0, axis_index_group...  11.8 us
    all_to_all x1, starting transfers between devices, second_fetch(): lax.all_to_all(sent, 'sub', split_axis=0, concat_axis=0, axis_index_group...  5.27 us
    ppermute x3, starting transfers between devices, turn(): parts.append(lax.ppermute(array, ('sub', 'blk'), pairs))  5.17 us
  transfers between devices with their start and end apart: 27, of which 14 were waited for; matrix products, arithmetic and copies ran while one was open for 4% of the time, Pallas kernels for 4%

profile of v1, /device:TPU:0, one launch (start us, length us, event | category | flops | bytes accessed | tf_op | source)
XLA Modules:
  0.0 178.5 jit_solution(16063863818646851722)
XLA Ops:
  0.6 2.5 %slice_bitcast_fusion = bf16[1280,512]{1,0:T(8,128)(2,1)} fusion(bf16[1,2048,512]{2,1,0:T(8,128)(2,1)} %param.12), kind=kLoop, calls=%fused_computation | loop fusion | bytes 2621440 | tf_op jit(solution)/shard_map/slice | solution.py:48
  3.1 1.7 collective-permute-start.1
  4.9 1.3 broadcast_in_dim.87
  6.3 12.0 %all-to-all-start = ((bf16[32,48,512]{2,1,0:T(8,128)(2,1)}), bf16[32,48,512]{2,1,0:T(8,128)(2,1)}, u32[]{:S(2)}, u32[]{:S(2)}) async-start(bf16[32,48,512]{2,1,0:T(8,128)(2,1)} %broadcast_in_dim.87), calls=%async_computation | async-start | bytes 3145728 | tf_op jit(solution)/shard_map/all_to_all | solution.py:280
  18.6 1.3 collective-permute-start.11
  19.9 1.3 collective-permute-start.10
  21.2 1.3 collective-permute-start.8
  22.5 1.3 collective-permute-start.5
  23.8 3.0 %collective-permute-done.11.m3 = f32[72,512]{1,0:T(8,128)S(1)} collective-permute-done((f32[72,512]{1,0:T(8,128)S(1)}, f32[72,512]{1,0:T(8,128)S(1)}, u32[]{:S(2)}, u32[]{:S(2)}) %collective-permute-start.11) | collective-permute-done | bytes 147488 | tf_op jit(solution)/shard_map/ppermute | solution.py:21
  30.5 25.9 %collective-permute-done.9.m1 = f32[72,512]{1,0:T(8,128)S(1)} collective-permute-done((f32[72,512]{1,0:T(8,128)S(1)}, f32[72,512]{1,0:T(8,128)S(1)}, u32[]{:S(2)}, u32[]{:S(2)}) %collective-permute-start.9) | collective-permute-done | bytes 147488 | tf_op jit(solution)/shard_map/ppermute | solution.py:21
  59.3 1.6 collective-permute-start.3
  63.0 6.7 %collective-permute-done.7.s2_in = bf16[8,64,512]{2,1,0:T(8,128)(2,1)} collective-permute-done((bf16[8,64,512]{2,1,0:T(8,128)(2,1)S(1)}, bf16[8,64,512]{2,1,0:T(8,128)(2,1)}, u32[]{:S(2)}, u32[]{:S(2)}) %collective-permute-start.7) | collective-permute-done | bytes 524320 | tf_op jit(solution)/shard_map/ppermute | solution.py:21
  71.2 1.4 slice.103
  72.6 1.3 collective-permute-start.4
  74.6 11.7 %collective-permute-done.6.s1_in = bf16[8,64,512]{2,1,0:T(8,128)(2,1)} collective-permute-done((bf16[8,64,512]{2,1,0:T(8,128)(2,1)S(1)}, bf16[8,64,512]{2,1,0:T(8,128)(2,1)}, u32[]{:S(2)}, u32[]{:S(2)}) %collective-permute-start.6) | collective-permute-done | bytes 524320 | tf_op jit(solution)/shard_map/ppermute | solution.py:21
  88.4 4.9 %collective-permute-done.14.w3 = bf16[32,512]{1,0:T(8,128)(2,1)S(1)} collective-permute-done((bf16[32,512]{1,0:T(8,128)(2,1)S(1)}, bf16[32,512]{1,0:T(8,128)(2,1)S(1)}, u32[]{:S(2)}, u32[]{:S(2)}) %collective-permute-start.14) | collective-permute-done | bytes 32800 | tf_op jit(solution)/shard_map/ppermute | solution.py:21
  95.3 5.2 %collective-permute-done.13.w2 = bf16[32,512]{1,0:T(8,128)(2,1)S(1)} collective-permute-done((bf16[32,512]{1,0:T(8,128)(2,1)S(1)}, bf16[32,512]{1,0:T(8,128)(2,1)S(1)}, u32[]{:S(2)}, u32[]{:S(2)}) %collective-permute-start.13) | collective-permute-done | bytes 32800 | tf_op jit(solution)/shard_map/ppermute | solution.py:21
  101.9 4.5 %collective-permute-done.12.w1 = bf16[32,512]{1,0:T(8,128)(2,1)S(1)} collective-permute-done((bf16[32,512]{1,0:T(8,128)(2,1)S(1)}, bf16[32,512]{1,0:T(8,128)(2,1)S(1)}, u32[]{:S(2)}, u32[]{:S(2)}) %collective-permute-start.12) | collective-permute-done | bytes 32800 | tf_op jit(solution)/shard_map/ppermute | solution.py:21
  106.4 21.4 %shard_map.104 = (bf16[4,32,512]{2,1,0:T(8,128)(2,1)S(1)}, bf16[5120,2048]{1,0:T(8,128)(2,1)}, f32[2560,2048]{1,0:T(8,128)}) custom-call(s32[3]{0:T(128)S(1)} %pad_add_fusion.meta, bf16[2048,512]{1,0:T(8,128)(2,1)S(1)} %bitcast.58, bf16[2048,512]{1,0:T(8,128)(2,1)} %collective-permute-done.a1_in, bf16[1280,512]{1,0:T(8,128)(2,1)} %collective-permute-done.2.a2_in, ...), custom_call_target="tpu_custom_call" | custom-call | flops 12884901888 | bytes 12582912 | tf_op jit(solution)/shard_map/pallas_call | solution.py:263
  129.1 1.3 collective-permute-start.16
  132.0 1.3 collective-permute-done.15
  135.6 5.3 %all-to-all-start.1 = ((bf16[16,32,512]{2,1,0:T(8,128)(2,1)}), bf16[16,32,512]{2,1,0:T(8,128)(2,1)S(1)}, u32[]{:S(2)}, u32[]{:S(2)}) async-start(bf16[16,32,512]{2,1,0:T(8,128)(2,1)} %select_select_fusion), calls=%async_computation.1 | async-start | bytes 1048576 | tf_op jit(solution)/shard_map/all_to_all | solution.py:307
  140.9 11.8 %all-to-all-done.1 = bf16[16,32,512]{2,1,0:T(8,128)(2,1)S(1)} async-done(((bf16[16,32,512]{2,1,0:T(8,128)(2,1)}), bf16[16,32,512]{2,1,0:T(8,128)(2,1)S(1)}, u32[]{:S(2)}, u32[]{:S(2)}) %all-to-all-start.1) | async-done | bytes 524320 | tf_op jit(solution)/shard_map/all_to_all | solution.py:307
  152.9 2.3 %collective-permute-start.21 = (bf16[32,512]{1,0:T(8,128)(2,1)S(1)}, bf16[32,512]{1,0:T(8,128)(2,1)S(1)}, u32[]{:S(2)}, u32[]{:S(2)}) collective-permute-start(bf16[32,512]{1,0:T(8,128)(2,1)S(1)} %fusion.10.v0), channel_id=1, source_target_pairs={{3,0},{0,1},{1,2},{2,3},{7,4},{4,5},{5,6},{6,7},{11,8},{8,9},{9,10... | collective-permute-start | bytes 98312 | tf_op jit(solution)/shard_map/ppermute | solution.py:32
  155.6 2.5 %collective-permute-start.19 = (bf16[32,512]{1,0:T(8,128)(2,1)S(1)}, bf16[32,512]{1,0:T(8,128)(2,1)S(1)}, u32[]{:S(2)}, u32[]{:S(2)}) collective-permute-start(bf16[32,512]{1,0:T(8,128)(2,1)S(1)} %fusion.10.v0), channel_id=1, source_target_pairs={{1,0},{2,1},{3,2},{0,3},{5,4},{6,5},{7,6},{4,7},{9,8},{10,9},{11,1... | collective-permute-start | bytes 98312 | tf_op jit(solution)/shard_map/ppermute | solution.py:32
  158.1 7.4 %shard_map.105 = (bf16[1024,128]{1,0:T(8,128)(2,1)S(1)}, f32[512,128]{1,0:T(8,128)S(1)}, f32[64,2048]{1,0:T(8,128)S(1)}) custom-call(s32[3]{0:T(128)S(1)} %pad_add_fusion.meta, bf16[5120,2048]{1,0:T(8,128)(2,1)} %get-tuple-element.8.response_in.response, f32[2560,2048]{1,0:T(8,128)} %get-tuple-element.9.history_in), custom_call_target="tpu_custom_call" | custom-call | flops 1073741824 | bytes 12582912 | tf_op jit(solution)/shard_map/pallas_call | solution.py:263
  165.5 3.2 %shard_map.106 = f32[4,96,512]{2,1,0:T(8,128)S(1)} custom-call(s32[3]{0:T(128)S(1)} %pad_add_fusion.meta, bf16[5120,2048]{1,0:T(8,128)(2,1)} %get-tuple-element.8.response_in.response, bf16[1024,128]{1,0:T(8,128)(2,1)S(1)} %get-tuple-element.10.at_ports, f32[512,128]{1,0:T(8,128)S(1)} %get-tuple-element.11.samples, f32[64,2048]{1,0:T(8,128)S(1)} %get-tuple-element.12.last, ...), custom_call_target="tpu_custom_call" | custom-call | flops 268435456 | bytes 12582912 | tf_op jit(solution)/shard_map/pallas_call | solution.py:263
  168.8 1.4 collective-permute-start.22
  170.2 2.4 %collective-permute-start.24 = (f32[96,512]{1,0:T(8,128)S(1)}, f32[96,512]{1,0:T(8,128)S(1)}, u32[]{:S(2)}, u32[]{:S(2)}) collective-permute-start(f32[96,512]{1,0:T(8,128)S(1)} %get-tuple-element.17), channel_id=1, source_target_pairs={{0,3},{6,5},{8,11},{14,13},{16,19},{22,21},{24,27},{30,29},{32,35}... | collective-permute-start | bytes 589832 | tf_op jit(solution)/shard_map/ppermute | solution.py:21
  172.6 1.3 collective-permute-start.23
  174.0 1.8 %collective-permute-done.24 = f32[96,512]{1,0:T(8,128)S(1)} collective-permute-done((f32[96,512]{1,0:T(8,128)S(1)}, f32[96,512]{1,0:T(8,128)S(1)}, u32[]{:S(2)}, u32[]{:S(2)}) %collective-permute-start.24) | collective-permute-done | bytes 196640 | tf_op jit(solution)/shard_map/ppermute | solution.py:21
  175.8 1.3 collective-permute-done.23
  (80 shorter events, 23.0 us)
Async XLA Ops:
  3.1 57.7 %collective-permute-start.1 = (bf16[1280,512]{1,0:T(8,128)(2,1)}, bf16[1280,512]{1,0:T(8,128)(2,1)}, u32[]{:S(2)}, u32[]{:S(2)}) collective-permute-start(bf16[1280,512]{1,0:T(8,128)(2,1)} %slice_bitcast_fusion), channel_id=1, source_target_pairs={{2,1},{4,7},{10,9},{12,15},{18,17},{20,23},{26,25},{28,31},{34,33}... | collective-permute-start | bytes 3932168 | tf_op jit(solution)/shard_map/ppermute | solution.py:21
  6.3 15.0 %copy-start.1 = (bf16[1,8,64,512]{3,2,1,0:T(8,128)(2,1)S(1)}, bf16[1,8,64,512]{3,2,1,0:T(8,128)(2,1)}, u32[]{:S(2)}) copy-start(bf16[1,8,64,512]{3,2,1,0:T(8,128)(2,1)} %param.10) | copy-start | bytes 1572868
  6.3 16.3 %copy-start = (bf16[1,2048,512]{2,1,0:T(8,128)(2,1)S(1)}, bf16[1,2048,512]{2,1,0:T(8,128)(2,1)}, u32[]{:S(2)}) copy-start(bf16[1,2048,512]{2,1,0:T(8,128)(2,1)} %param.12) | copy-start | bytes 6291460
  6.3 56.5 %copy-start.9 = (s32[32]{0:T(128)S(1)}, s32[32]{0:T(128)}, u32[]{:S(2)}) copy-start(s32[32]{0:T(128)} %param.17) | copy-start | bytes 388
  6.3 64.9 %all-to-all-start = ((bf16[32,48,512]{2,1,0:T(8,128)(2,1)}), bf16[32,48,512]{2,1,0:T(8,128)(2,1)}, u32[]{:S(2)}, u32[]{:S(2)}) async-start(bf16[32,48,512]{2,1,0:T(8,128)(2,1)} %broadcast_in_dim.87), calls=%async_computation | async-start | bytes 3145728 | tf_op jit(solution)/shard_map/all_to_all | solution.py:280
  18.6 8.2 %collective-permute-start.11 = (f32[72,512]{1,0:T(8,128)S(1)}, f32[72,512]{1,0:T(8,128)S(1)}, u32[]{:S(2)}, u32[]{:S(2)}) collective-permute-start(f32[72,512]{1,0:T(8,128)S(1)} %maximum_maximum_fusion.m0), channel_id=1, source_target_pairs={{3,0},{5,6},{11,8},{13,14},{19,16},{21,22},{27,24},{29,30},{35,32}... | collective-permute-start | bytes 442376 | tf_op jit(solution)/shard_map/ppermute | solution.py:21
  19.9 8.6 %collective-permute-start.10 = (f32[72,512]{1,0:T(8,128)S(1)}, f32[72,512]{1,0:T(8,128)S(1)}, u32[]{:S(2)}, u32[]{:S(2)}) collective-permute-start(f32[72,512]{1,0:T(8,128)S(1)} %maximum_maximum_fusion.m0), channel_id=1, source_target_pairs={{2,0},{4,6},{10,8},{12,14},{18,16},{20,22},{26,24},{28,30},{34,32}... | collective-permute-start | bytes 442376 | tf_op jit(solution)/shard_map/ppermute | solution.py:21
  21.2 38.0 %collective-permute-start.8 = (bf16[8,64,512]{2,1,0:T(8,128)(2,1)S(1)}, bf16[8,64,512]{2,1,0:T(8,128)(2,1)S(1)}, u32[]{:S(2)}, u32[]{:S(2)}) collective-permute-start(bf16[8,64,512]{2,1,0:T(8,128)(2,1)S(1)} %bitcast.63), channel_id=1, source_target_pairs={{3,0},{5,6},{11,8},{13,14},{19,16},{21,22},{27,24},{29,30},{35,32}... | collective-permute-start | bytes 1572872 | tf_op jit(solution)/shard_map/ppermute | solution.py:21
  22.5 83.8 %collective-permute-start.5 = (bf16[2048,512]{1,0:T(8,128)(2,1)S(1)}, bf16[2048,512]{1,0:T(8,128)(2,1)}, u32[]{:S(2)}, u32[]{:S(2)}) collective-permute-start(bf16[2048,512]{1,0:T(8,128)(2,1)S(1)} %bitcast.56), channel_id=1, source_target_pairs={{3,0},{5,6},{11,8},{13,14},{19,16},{21,22},{27,24},{29,30},{35,32}... | collective-permute-start | bytes 6291464 | tf_op jit(solution)/shard_map/ppermute | solution.py:21
  26.9 79.5 %collective-permute-start = (bf16[2048,512]{1,0:T(8,128)(2,1)S(1)}, bf16[2048,512]{1,0:T(8,128)(2,1)}, u32[]{:S(2)}, u32[]{:S(2)}) collective-permute-start(bf16[2048,512]{1,0:T(8,128)(2,1)S(1)} %bitcast.57), channel_id=1, source_target_pairs={{1,0},{7,6},{9,8},{15,14},{17,16},{23,22},{25,24},{31,30},{33,32},... | collective-permute-start | bytes 6291464 | tf_op jit(solution)/shard_map/ppermute | solution.py:21
  29.2 27.2 %collective-permute-start.9 = (f32[72,512]{1,0:T(8,128)S(1)}, f32[72,512]{1,0:T(8,128)S(1)}, u32[]{:S(2)}, u32[]{:S(2)}) collective-permute-start(f32[72,512]{1,0:T(8,128)S(1)} %maximum_maximum_fusion.m0), channel_id=1, source_target_pairs={{1,0},{7,6},{9,8},{15,14},{17,16},{23,22},{25,24},{31,30},{33,32},... | collective-permute-start | bytes 442376 | tf_op jit(solution)/shard_map/ppermute | solution.py:21
  57.0 12.7 %collective-permute-start.7 = (bf16[8,64,512]{2,1,0:T(8,128)(2,1)S(1)}, bf16[8,64,512]{2,1,0:T(8,128)(2,1)}, u32[]{:S(2)}, u32[]{:S(2)}) collective-permute-start(bf16[8,64,512]{2,1,0:T(8,128)(2,1)S(1)} %bitcast.64), channel_id=1, source_target_pairs={{2,0},{4,6},{10,8},{12,14},{18,16},{20,22},{26,24},{28,30},{34,32}... | collective-permute-start | bytes 1572872 | tf_op jit(solution)/shard_map/ppermute | solution.py:21
  59.3 13.3 %collective-permute-start.3 = (bf16[768,512]{1,0:T(8,128)(2,1)}, bf16[768,512]{1,0:T(8,128)(2,1)}, u32[]{:S(2)}, u32[]{:S(2)}) collective-permute-start(bf16[768,512]{1,0:T(8,128)(2,1)} %slice_bitcast_fusion.1), channel_id=1, source_target_pairs={{2,3},{4,5},{10,11},{12,13},{18,19},{20,21},{26,27},{28,29},{34,35... | collective-permute-start | bytes 2359304 | tf_op jit(solution)/shard_map/ppermute | solution.py:21
  60.8 45.5 %collective-permute-start.2 = (bf16[1280,512]{1,0:T(8,128)(2,1)}, bf16[1280,512]{1,0:T(8,128)(2,1)}, u32[]{:S(2)}, u32[]{:S(2)}) collective-permute-start(bf16[1280,512]{1,0:T(8,128)(2,1)} %collective-permute-done.1), channel_id=1, source_target_pairs={{1,0},{7,6},{9,8},{15,14},{17,16},{23,22},{25,24},{31,30},{33,32},... | collective-permute-start | bytes 3932168 | tf_op jit(solution)/shard_map/ppermute | solution.py:21
  69.7 16.5 %collective-permute-start.6 = (bf16[8,64,512]{2,1,0:T(8,128)(2,1)S(1)}, bf16[8,64,512]{2,1,0:T(8,128)(2,1)}, u32[]{:S(2)}, u32[]{:S(2)}) collective-permute-start(bf16[8,64,512]{2,1,0:T(8,128)(2,1)S(1)} %bitcast.65), channel_id=1, source_target_pairs={{1,0},{7,6},{9,8},{15,14},{17,16},{23,22},{25,24},{31,30},{33,32},... | collective-permute-start | bytes 1572872 | tf_op jit(solution)/shard_map/ppermute | solution.py:21
  71.2 35.2 %copy-start.3 = (f32[72,512]{1,0:T(8,128)S(1)}, f32[72,512]{1,0:T(8,128)}, u32[]{:S(2)}) copy-start(f32[72,512]{1,0:T(8,128)} %copy-done.2) | copy-start | bytes 442372
  71.2 35.2 %copy-start.5 = (f32[72,512]{1,0:T(8,128)S(1)}, f32[72,512]{1,0:T(8,128)}, u32[]{:S(2)}) copy-start(f32[72,512]{1,0:T(8,128)} %copy-done.4) | copy-start | bytes 442372
  72.6 33.8 %collective-permute-start.4 = (bf16[768,512]{1,0:T(8,128)(2,1)}, bf16[768,512]{1,0:T(8,128)(2,1)S(1)}, u32[]{:S(2)}, u32[]{:S(2)}) collective-permute-start(bf16[768,512]{1,0:T(8,128)(2,1)} %collective-permute-done.3), channel_id=1, source_target_pairs={{3,0},{5,6},{11,8},{13,14},{19,16},{21,22},{27,24},{29,30},{35,32}... | collective-permute-start | bytes 2359304 | tf_op jit(solution)/shard_map/ppermute | solution.py:21
  86.2 7.0 %collective-permute-start.14 = (bf16[32,512]{1,0:T(8,128)(2,1)S(1)}, bf16[32,512]{1,0:T(8,128)(2,1)S(1)}, u32[]{:S(2)}, u32[]{:S(2)}) collective-permute-start(bf16[32,512]{1,0:T(8,128)(2,1)S(1)} %bitcast.59), channel_id=1, source_target_pairs={{3,0},{5,6},{11,8},{13,14},{19,16},{21,22},{27,24},{29,30},{35,32}... | collective-permute-start | bytes 98312 | tf_op jit(solution)/shard_map/ppermute | solution.py:21
  93.2 7.3 %collective-permute-start.13 = (bf16[32,512]{1,0:T(8,128)(2,1)S(1)}, bf16[32,512]{1,0:T(8,128)(2,1)S(1)}, u32[]{:S(2)}, u32[]{:S(2)}) collective-permute-start(bf16[32,512]{1,0:T(8,128)(2,1)S(1)} %bitcast.60), channel_id=1, source_target_pairs={{2,0},{4,6},{10,8},{12,14},{18,16},{20,22},{26,24},{28,30},{34,32}... | collective-permute-start | bytes 98312 | tf_op jit(solution)/shard_map/ppermute | solution.py:21
  100.6 5.8 %collective-permute-start.12 = (bf16[32,512]{1,0:T(8,128)(2,1)S(1)}, bf16[32,512]{1,0:T(8,128)(2,1)S(1)}, u32[]{:S(2)}, u32[]{:S(2)}) collective-permute-start(bf16[32,512]{1,0:T(8,128)(2,1)S(1)} %bitcast.61), channel_id=1, source_target_pairs={{1,0},{7,6},{9,8},{15,14},{17,16},{23,22},{25,24},{31,30},{33,32},... | collective-permute-start | bytes 98312 | tf_op jit(solution)/shard_map/ppermute | solution.py:21
  127.8 3.9 %collective-permute-start.17 = (bf16[32,512]{1,0:T(8,128)(2,1)S(1)}, bf16[32,512]{1,0:T(8,128)(2,1)S(1)}, u32[]{:S(2)}, u32[]{:S(2)}) collective-permute-start(bf16[32,512]{1,0:T(8,128)(2,1)S(1)} %get-tuple-element.19), channel_id=1, source_target_pairs={{0,3},{6,5},{8,11},{14,13},{16,19},{22,21},{24,27},{30,29},{32,35}... | collective-permute-start | bytes 98312 | tf_op jit(solution)/shard_map/ppermute | solution.py:21
  129.1 2.9 %collective-permute-start.16 = (bf16[32,512]{1,0:T(8,128)(2,1)S(1)}, bf16[32,512]{1,0:T(8,128)(2,1)S(1)}, u32[]{:S(2)}, u32[]{:S(2)}) collective-permute-start(bf16[32,512]{1,0:T(8,128)(2,1)S(1)} %get-tuple-element.20), channel_id=1, source_target_pairs={{0,2},{6,4},{8,10},{14,12},{16,18},{22,20},{24,26},{30,28},{32,34}... | collective-permute-start | bytes 98312 | tf_op jit(solution)/shard_map/ppermute | solution.py:21
  130.4 2.9 %collective-permute-start.15 = (bf16[32,512]{1,0:T(8,128)(2,1)S(1)}, bf16[32,512]{1,0:T(8,128)(2,1)S(1)}, u32[]{:S(2)}, u32[]{:S(2)}) collective-permute-start(bf16[32,512]{1,0:T(8,128)(2,1)S(1)} %get-tuple-element.21), channel_id=1, source_target_pairs={{0,1},{6,7},{8,9},{14,15},{16,17},{22,23},{24,25},{30,31},{32,33},... | collective-permute-start | bytes 98312 | tf_op jit(solution)/shard_map/ppermute | solution.py:21
  133.3 1.3 collective-permute-start.18
  135.6 17.1 %all-to-all-start.1 = ((bf16[16,32,512]{2,1,0:T(8,128)(2,1)}), bf16[16,32,512]{2,1,0:T(8,128)(2,1)S(1)}, u32[]{:S(2)}, u32[]{:S(2)}) async-start(bf16[16,32,512]{2,1,0:T(8,128)(2,1)} %select_select_fusion), calls=%async_computation.1 | async-start | bytes 1048576 | tf_op jit(solution)/shard_map/all_to_all | solution.py:307
  152.9 12.5 %collective-permute-start.21 = (bf16[32,512]{1,0:T(8,128)(2,1)S(1)}, bf16[32,512]{1,0:T(8,128)(2,1)S(1)}, u32[]{:S(2)}, u32[]{:S(2)}) collective-permute-start(bf16[32,512]{1,0:T(8,128)(2,1)S(1)} %fusion.10.v0), channel_id=1, source_target_pairs={{3,0},{0,1},{1,2},{2,3},{7,4},{4,5},{5,6},{6,7},{11,8},{8,9},{9,10... | collective-permute-start | bytes 98312 | tf_op jit(solution)/shard_map/ppermute | solution.py:32
  155.3 10.2 %collective-permute-start.20 = (bf16[32,512]{1,0:T(8,128)(2,1)S(1)}, bf16[32,512]{1,0:T(8,128)(2,1)S(1)}, u32[]{:S(2)}, u32[]{:S(2)}) collective-permute-start(bf16[32,512]{1,0:T(8,128)(2,1)S(1)} %fusion.10.v0), channel_id=1, source_target_pairs={{2,0},{3,1},{0,2},{1,3},{6,4},{7,5},{4,6},{5,7},{10,8},{11,9},{8,1... | collective-permute-start | bytes 98312 | tf_op jit(solution)/shard_map/ppermute | solution.py:32
  155.6 9.9 %collective-permute-start.19 = (bf16[32,512]{1,0:T(8,128)(2,1)S(1)}, bf16[32,512]{1,0:T(8,128)(2,1)S(1)}, u32[]{:S(2)}, u32[]{:S(2)}) collective-permute-start(bf16[32,512]{1,0:T(8,128)(2,1)S(1)} %fusion.10.v0), channel_id=1, source_target_pairs={{1,0},{2,1},{3,2},{0,3},{5,4},{6,5},{7,6},{4,7},{9,8},{10,9},{11,1... | collective-permute-start | bytes 98312 | tf_op jit(solution)/shard_map/ppermute | solution.py:32
  168.8 5.2 %collective-permute-start.22 = (f32[96,512]{1,0:T(8,128)S(1)}, f32[96,512]{1,0:T(8,128)S(1)}, u32[]{:S(2)}, u32[]{:S(2)}) collective-permute-start(f32[96,512]{1,0:T(8,128)S(1)} %get-tuple-element.16), channel_id=1, source_target_pairs={{0,1},{6,7},{8,9},{14,15},{16,17},{22,23},{24,25},{30,31},{32,33},... | collective-permute-start | bytes 589832 | tf_op jit(solution)/shard_map/ppermute | solution.py:21
  170.2 5.6 %collective-permute-start.24 = (f32[96,512]{1,0:T(8,128)S(1)}, f32[96,512]{1,0:T(8,128)S(1)}, u32[]{:S(2)}, u32[]{:S(2)}) collective-permute-start(f32[96,512]{1,0:T(8,128)S(1)} %get-tuple-element.17), channel_id=1, source_target_pairs={{0,3},{6,5},{8,11},{14,13},{16,19},{22,21},{24,27},{30,29},{32,35}... | collective-permute-start | bytes 589832 | tf_op jit(solution)/shard_map/ppermute | solution.py:21
  172.6 4.5 %collective-permute-start.23 = (f32[96,512]{1,0:T(8,128)S(1)}, f32[96,512]{1,0:T(8,128)S(1)}, u32[]{:S(2)}, u32[]{:S(2)}) collective-permute-start(f32[96,512]{1,0:T(8,128)S(1)} %get-tuple-element.18), channel_id=1, source_target_pairs={{0,2},{6,4},{8,10},{14,12},{16,18},{22,20},{24,26},{30,28},{32,34}... | collective-permute-start | bytes 589832 | tf_op jit(solution)/shard_map/ppermute | solution.py:21
  (7 other events, 50.4 us)

commit v2 on v1

--- a/solution.py
+++ b/solution.py
@@ -73,15 +73,16 @@
     return jnp.dot(operand[...], matrix[...], preferred_element_type=F32)
 
 
-DIAG = 64
-INJECT = 65
+DIAG = 0
+INJECT = 1
 
 
 def sweep_kernel(meta, a0_in, a1_in, a2_in, a3_in, a4_in, s0_in, s1_in, s2_in, s3_in, m0, m1, m2, m3, w0, w1, w2, w3,
                  out, response_out, history_out, operand, state, forced, response, history,
                  sent, a0, a1, a2, a3, a4, s0, s1, s2, s3, arrived):
-    steps, cases, block = s0.shape
-    ports = w0.shape[0]
+    later_steps, cases, block = s0.shape
+    steps = later_steps + 1
+    ports = w0.shape[0] - cases
     all_ports = SLOTS * ports
     nodes = SLOTS * block
     count, spacing, place = meta[0], meta[1], meta[2]
@@ -96,7 +97,7 @@
         load.start()
     marks = port_rows(all_ports, nodes)
     spread = jnp.where(marks, 1.0, 0.0).astype(BF16)
-    waves = jnp.concatenate([w[...] for w in (w0, w1, w2, w3)], axis=0).astype(F32)
+    waves = jnp.concatenate([w[:ports, :] for w in (w0, w1, w2, w3)], axis=0).astype(F32)
     waves = jnp.transpose(waves).astype(BF16)
     forced[...] = jnp.dot(waves, spread, preferred_element_type=F32).astype(BF16)
     state[...] = jnp.where(marks, 1.0, 0.0)
@@ -105,15 +106,13 @@
         rows = pl.ds(pl.multiple_of(fine * cases, cases), cases)
         lanes = slice(d * block, (d + 1) * block)
         drive = miscs[d][INJECT : INJECT + 1, :] * forced[rows, lanes].astype(F32)
-        return (current + spacing_float * (sources[d][fine].astype(F32) + drive)).astype(BF16)
+        return (current + spacing_float * (sources[d][fine - 1].astype(F32) + drive)).astype(BF16)
 
     def spot(d):
         return pl.ds(pl.multiple_of(lax.rem(place + d, SLOTS) * block, block), block)
 
-    for load in loads[:SLOTS]:
-        load.wait()
-    for d in range(SLOTS):
-        operand[0, :cases, spot(d)] = argument(miscs[d][:cases, :], spacing - 1, d)
+    for d, late in enumerate((w0, w1, w2, w3)):
+        operand[0, :cases, spot(d)] = late[ports:, :]
         operand[0, cases:, spot(d)] = spread[:, d * block : (d + 1) * block]
 
     def send(k):
@@ -147,6 +146,8 @@
             copy.start()
         return carry
 
+    for load in loads[:SLOTS]:
+        load.wait()
     step(jnp.int32(0), None)
     lax.fori_loop(1, count, step, 0)
 
@@ -272,24 +273,50 @@
     )(meta, *operands)
 
 
-def first_fetch(waves, partner, position_of):
+def same_core(subs):
+    return [[s for s in range(subs) if s % 2 == core] for core in (0, 1)]
+
+
+def locate(ids, position_of):
+    identities = jnp.arange(position_of.shape[0], dtype=jnp.int32)
+    return jnp.sum(jnp.where(ids[..., None] == identities, position_of, 0), axis=-1, dtype=jnp.int32)
+
+
+def first_exchange(waves):
+    copies = jnp.broadcast_to(waves, (lax.axis_size("sub"), *waves.shape))
+    return lax.all_to_all(copies, "sub", split_axis=0, concat_axis=0, tiled=True)
+
+
+def prepare_kernel(meta, located, everyone, state, injects, source, late, before, turned, row, sem):
+    subs, ports, _ = everyone.shape
+    cases, block = state.shape
+    spacing = meta[1]
+    start = spacing - 1
+    load = pltpu.make_async_copy(source.at[start], row, sem)
+    load.start()
+    picked = jnp.zeros(before.shape, F32)
+    for sub in range(subs):
+        picked = jnp.where(located[...] == sub, everyone[sub].astype(F32), picked)
+    before[...] = picked
+    turned[:, :ports] = jnp.transpose(picked)
+    waves = turned[pl.ds(pl.multiple_of(start * cases, cases), cases), :ports].astype(BF16)
+    spread = jnp.where(port_rows(ports, block), 1.0, 0.0).astype(BF16)
+    drive = injects[...] * jnp.dot(waves, spread, preferred_element_type=F32)
+    load.wait()
+    operand = state[...] + spacing.astype(F32) * (row[...].astype(F32) + drive)
+    late[:ports, :] = picked.astype(BF16)
+    late[ports:, :] = operand.astype(BF16)
+
+
+def requests(partner, position_of):
     subs = lax.axis_size("sub")
-    ports = waves.shape[0]
-    ids = jnp.pad(partner.astype(BF16)[None, :], ((0, 15), (0, waves.shape[1] - ports)))
-    copies = jnp.broadcast_to(jnp.concatenate([waves, ids], axis=0), (subs, ports + 16, waves.shape[1]))
-    everyone = lax.all_to_all(copies, "sub", split_axis=0, concat_axis=0, tiled=True)
-    identities = jnp.arange(subs, dtype=jnp.int32)
-
-    def locate(ids):
-        return jnp.sum(
-            jnp.where(ids[..., None] == identities, position_of, 0), axis=-1, dtype=jnp.int32
-        )
-
-    selector = (locate(partner)[:, None] == identities[None, :]).astype(BF16)
-    incoming = jnp.einsum(
-        "jr,rjc->jc", selector, everyone[:, :ports], preferred_element_type=F32
-    )
-    return incoming, locate(everyone[:, ports, :ports].astype(jnp.int32))
+    ports = partner.shape[0]
+    ids = jnp.pad(partner.astype(BF16)[None, :], ((0, 15), (0, 128 - ports)))
+    copies = jnp.broadcast_to(ids, (subs // 2, *ids.shape))
+    everyone = lax.all_to_all(
+        copies, "sub", split_axis=0, concat_axis=0, axis_index_groups=same_core(subs), tiled=True
+    )
+    return locate(everyone[:, 0, :ports].astype(jnp.int32), position_of)
 
 
 def second_fetch(waves, located):
@@ -297,15 +324,13 @@
     sub = lax.axis_index("sub")
     swap = [(s * SLOTS + r, (s ^ 1) * SLOTS + r) for s in range(subs) for r in range(SLOTS)]
     others = lax.ppermute(waves, ("sub", "blk"), swap)
-    pairs = located.reshape(subs // 2, 2, -1)
-    wanted = jnp.where(lax.rem(sub, 2) == 0, pairs[:, 0], pairs[:, 1])[:, :, None]
+    wanted = located[:, :, None]
     zero = jnp.zeros((), BF16)
     sent = jnp.where(
         wanted == sub, waves[None], jnp.where(wanted == (sub ^ 1), others[None], zero)
     )
-    groups = [[s for s in range(subs) if s % 2 == core] for core in (0, 1)]
     parts = lax.all_to_all(
-        sent, "sub", split_axis=0, concat_axis=0, axis_index_groups=groups, tiled=True
+        sent, "sub", split_axis=0, concat_axis=0, axis_index_groups=same_core(subs), tiled=True
     )
     return jnp.sum(parts.astype(F32), axis=0)
 
@@ -323,15 +348,28 @@
     count = jnp.where(bucket == 0, steps // 4, jnp.where(bucket == 1, steps // 2, steps))
     spacing = steps // count
     meta = jnp.concatenate([count, spacing, x[None]]).astype(jnp.int32)
+    home_meta = jnp.concatenate([jnp.where(rel == 0, count, 1), meta[1:]])
 
     matrices = gather_matrix(matrix)
     injects = jnp.pad(coupling[0][:, None], ((0, 0), (0, block // ports - 1))).reshape(1, block)
-    misc = jnp.concatenate([state, inverse_diag, injects, jnp.zeros((6, block), F32)], axis=0)
+    misc = jnp.concatenate([inverse_diag, injects, jnp.zeros((6, block), F32)], axis=0)
     miscs = to_home(misc)
-    sources = to_home(source)
-
-    before, located = first_fetch(initial_waves[0], partner[0], position_of)
-    incoming = to_home(before.astype(BF16))
+    sources = to_home(source[1:])
+    located = requests(partner[0], position_of)
+
+    shape = jax.ShapeDtypeStruct
+    everyone = first_exchange(initial_waves[0])
+    column = jnp.broadcast_to(
+        locate(partner[0], position_of)[:, None], (ports, steps * cases)
+    )
+    late, before = call(
+        prepare_kernel,
+        (shape((ports + cases, block), BF16), shape((ports, steps * cases), F32)),
+        [pltpu.VMEM((steps * cases, 128), F32), pltpu.VMEM((cases, block), BF16),
+         pltpu.SemaphoreType.DMA],
+        4 << 20, 8, meta, column, everyone, state, injects, source, hbm_ins=(4,),
+    )
+    incoming = to_home(late)
 
     shape = jax.ShapeDtypeStruct
     slots, response, history = call(
@@ -343,7 +381,7 @@
          pltpu.VMEM((steps * cases, nodes), F32), pltpu.SemaphoreType.DMA((2, steps)),
          *(pltpu.VMEM(m.shape, BF16) for m in matrices), *(pltpu.VMEM(a.shape, BF16) for a in sources),
          pltpu.SemaphoreType.DMA((9,))],
-        2 * steps * (cases + all_ports) * nodes * nodes, LIMITS[0], meta,
+        2 * steps * (cases + all_ports) * nodes * nodes, LIMITS[0], home_meta,
         *matrices, *sources, *miscs, *incoming, hbm_outs=(1, 2), hbm_ins=range(9),
     )
     at_ports, samples, last = call(

time: 180 us -> 176 us (0.978)
  waiting for transfers between devices: 80 us -> 69.1 us
  starting transfers between devices: 51.5 us -> 56.4 us
    ppermute x21, waiting for transfers between devices: 67 us -> 55.3 us  [hop(): return lax.ppermute(array, ('sub', 'blk'), pairs)]
    all_to_all x1 -> x2, starting transfers between devices: 12 us -> 15.5 us  [the longest x1 8.45 us: first_exchange(): lax.all_to_all(copies, 'sub', split_axis=0, concat_axis=0, tiled=True)]
    ppermute x21, starting transfers between devices: 29 us -> 30.9 us  [hop(): return lax.ppermute(array, ('sub', 'blk'), pairs)]
    pallas_call x3 -> x4, Pallas kernels: 32 us -> 33.7 us  [call(): pl.pallas_call(kernel, out_shape=outs, in_specs=[pl.BlockSpec(memory_spac...]
  transfers between devices with their start and end apart: 27 -> 28, of which waited for: 14 -> 13; matrix products, arithmetic and copies ran while one was open for 4% -> 3% of each run, Pallas kernels for 4% -> 5%
where the time goes in v2:
time: 176 us; the launch traced here: 174 us
  waiting for transfers between devices  69.1 us (39%)
  starting transfers between devices  56.4 us (32%)
  Pallas kernels  33.7 us (19%)
  local copies, waits for them, and re-layouts  9.44 us (5%)
  other arithmetic  3.4 us (2%)
  between operations  1.78 us (1%)
    ppermute x21, waiting for transfers between devices, hop(): return lax.ppermute(array, ('sub', 'blk'), pairs)  55.3 us
    pallas_call x4, Pallas kernels, call(): pl.pallas_call(kernel, out_shape=outs, in_specs=[pl.BlockSpec(memory_spac...  33.7 us
    ppermute x21, starting transfers between devices, hop(): return lax.ppermute(array, ('sub', 'blk'), pairs)  30.9 us
    all_to_all x1, waiting for transfers between devices, second_fetch(): lax.all_to_all(sent, 'sub', split_axis=0, concat_axis=0, axis_index_group...  11.8 us
    all_to_all x1, starting transfers between devices, first_exchange(): lax.all_to_all(copies, 'sub', split_axis=0, concat_axis=0, tiled=True)  8.45 us
    all_to_all x1, starting transfers between devices, requests(): lax.all_to_all(copies, 'sub', split_axis=0, concat_axis=0, axis_index_gro...  7.1 us
    all_to_all x1, starting transfers between devices, second_fetch(): lax.all_to_all(sent, 'sub', split_axis=0, concat_axis=0, axis_index_group...  5.38 us
    ppermute x3, starting transfers between devices, turn(): parts.append(lax.ppermute(array, ('sub', 'blk'), pairs))  4.49 us
  transfers between devices with their start and end apart: 28, of which 13 were waited for; matrix products, arithmetic and copies ran while one was open for 3% of the time, Pallas kernels for 5%

profile of v2, /device:TPU:0, one launch (start us, length us, event | category | flops | bytes accessed | tf_op | source)
XLA Modules:
  0.0 173.8 jit_solution(9031676822624875253)
XLA Ops:
  0.7 2.6 %slice_bitcast_fusion = bf16[1280,512]{1,0:T(8,128)(2,1)} fusion(bf16[1,2048,512]{2,1,0:T(8,128)(2,1)} %param.12), kind=kLoop, calls=%fused_computation | loop fusion | bytes 2621440 | tf_op jit(solution)/shard_map/slice | solution.py:48
  3.3 1.7 %collective-permute-start.1 = (bf16[1280,512]{1,0:T(8,128)(2,1)}, bf16[1280,512]{1,0:T(8,128)(2,1)}, u32[]{:S(2)}, u32[]{:S(2)}) collective-permute-start(bf16[1280,512]{1,0:T(8,128)(2,1)} %slice_bitcast_fusion), channel_id=1, source_target_pairs={{2,1},{4,7},{10,9},{12,15},{18,17},{20,23},{26,25},{28,31},{34,33}... | collective-permute-start | bytes 3932168 | tf_op jit(solution)/shard_map/ppermute | solution.py:21
  6.3 1.3 collective-permute-start.5
  8.0 1.3 collective-permute-start.10
  9.3 1.3 collective-permute-start.11
  11.4 6.0 %collective-permute-done.10.m2 = f32[8,512]{1,0:T(8,128)S(1)} collective-permute-done((f32[8,512]{1,0:T(8,128)S(1)}, f32[8,512]{1,0:T(8,128)S(1)}, u32[]{:S(2)}, u32[]{:S(2)}) %collective-permute-start.10) | collective-permute-done | bytes 16416 | tf_op jit(solution)/shard_map/ppermute | solution.py:21
  17.4 1.3 collective-permute-start.9
  18.7 17.1 %collective-permute-done.11.m3 = f32[8,512]{1,0:T(8,128)S(1)} collective-permute-done((f32[8,512]{1,0:T(8,128)S(1)}, f32[8,512]{1,0:T(8,128)S(1)}, u32[]{:S(2)}, u32[]{:S(2)}) %collective-permute-start.11) | collective-permute-done | bytes 16416 | tf_op jit(solution)/shard_map/ppermute | solution.py:21
  38.1 1.6 collective-permute-start.3
  40.7 8.4 %all-to-all-start = ((bf16[32,32,512]{2,1,0:T(8,128)(2,1)}), bf16[32,32,512]{2,1,0:T(8,128)(2,1)S(1)}, u32[]{:S(2)}, u32[]{:S(2)}) async-start(bf16[32,32,512]{2,1,0:T(8,128)(2,1)} %broadcast_in_dim.97), calls=%async_computation | async-start | bytes 2097152 | tf_op jit(solution)/shard_map/all_to_all | solution.py:287
  49.2 1.3 collective-permute-start.7
  50.5 1.3 collective-permute-start.2
  51.8 9.5 %collective-permute-done.7.s2_in = bf16[7,64,512]{2,1,0:T(8,128)(2,1)S(1)} collective-permute-done((bf16[7,64,512]{2,1,0:T(8,128)(2,1)}, bf16[7,64,512]{2,1,0:T(8,128)(2,1)S(1)}, u32[]{:S(2)}, u32[]{:S(2)}) %collective-permute-start.7) | collective-permute-done | bytes 458784 | tf_op jit(solution)/shard_map/ppermute | solution.py:21
  63.4 1.3 collective-permute-start.4
  68.6 5.4 %collective-permute-done.8.s3_in = bf16[7,64,512]{2,1,0:T(8,128)(2,1)} collective-permute-done((bf16[7,64,512]{2,1,0:T(8,128)(2,1)}, bf16[7,64,512]{2,1,0:T(8,128)(2,1)}, u32[]{:S(2)}, u32[]{:S(2)}) %collective-permute-start.8) | collective-permute-done | bytes 458784 | tf_op jit(solution)/shard_map/ppermute | solution.py:21
  75.9 7.1 %all-to-all-start.1 = ((bf16[16,16,128]{2,1,0:T(8,128)(2,1)}), bf16[16,16,128]{2,1,0:T(8,128)(2,1)S(1)}, u32[]{:S(2)}, u32[]{:S(2)}) async-start(bf16[16,16,128]{2,1,0:T(8,128)(2,1)} %broadcast_in_dim.98), calls=%async_computation.1 | async-start | bytes 131072 | tf_op jit(solution)/shard_map/all_to_all | solution.py:316
  83.1 1.3 collective-permute-start.13
  84.4 6.6 %collective-permute-done.13.w2 = bf16[96,512]{1,0:T(8,128)(2,1)S(1)} collective-permute-done((bf16[96,512]{1,0:T(8,128)(2,1)S(1)}, bf16[96,512]{1,0:T(8,128)(2,1)S(1)}, u32[]{:S(2)}, u32[]{:S(2)}) %collective-permute-start.13) | collective-permute-done | bytes 98336 | tf_op jit(solution)/shard_map/ppermute | solution.py:21
  92.4 6.4 %collective-permute-done.14.w3 = bf16[96,512]{1,0:T(8,128)(2,1)S(1)} collective-permute-done((bf16[96,512]{1,0:T(8,128)(2,1)S(1)}, bf16[96,512]{1,0:T(8,128)(2,1)S(1)}, u32[]{:S(2)}, u32[]{:S(2)}) %collective-permute-start.14) | collective-permute-done | bytes 98336 | tf_op jit(solution)/shard_map/ppermute | solution.py:21
  99.8 22.0 %shard_map.105 = (bf16[4,32,512]{2,1,0:T(8,128)(2,1)S(1)}, bf16[5120,2048]{1,0:T(8,128)(2,1)}, f32[2560,2048]{1,0:T(8,128)}) custom-call(s32[3]{0:T(128)S(1)} %add_add_fusion.1.meta, bf16[2048,512]{1,0:T(8,128)(2,1)S(1)} %bitcast.46, bf16[2048,512]{1,0:T(8,128)(2,1)} %collective-permute-done.a1_in, bf16[1280,512]{1,0:T(8,128)(2,1)} %collective-permute-done.2.a2_in, ...), custom_call_target="tpu_custom_call" | custom-call | flops 12884901888 | bytes 12582912 | tf_op jit(solution)/shard_map/pallas_call | solution.py:264
  121.9 1.3 collective-permute-start.15
  123.2 1.3 collective-permute-start.16
  124.5 1.3 collective-permute-start.17
  129.7 5.4 %all-to-all-start.2 = ((bf16[16,32,512]{2,1,0:T(8,128)(2,1)}), bf16[16,32,512]{2,1,0:T(8,128)(2,1)S(1)}, u32[]{:S(2)}, u32[]{:S(2)}) async-start(bf16[16,32,512]{2,1,0:T(8,128)(2,1)} %select_select_fusion), calls=%async_computation.2 | async-start | bytes 1048576 | tf_op jit(solution)/shard_map/all_to_all | solution.py:332
  135.1 11.8 %all-to-all-done.2 = bf16[16,32,512]{2,1,0:T(8,128)(2,1)S(1)} async-done(((bf16[16,32,512]{2,1,0:T(8,128)(2,1)}), bf16[16,32,512]{2,1,0:T(8,128)(2,1)S(1)}, u32[]{:S(2)}, u32[]{:S(2)}) %all-to-all-start.2) | async-done | bytes 524320 | tf_op jit(solution)/shard_map/all_to_all | solution.py:332
  147.1 3.5 %collective-permute-start.19 = (bf16[32,512]{1,0:T(8,128)(2,1)S(1)}, bf16[32,512]{1,0:T(8,128)(2,1)S(1)}, u32[]{:S(2)}, u32[]{:S(2)}) collective-permute-start(bf16[32,512]{1,0:T(8,128)(2,1)S(1)} %multiply_convert_fusion.v0), channel_id=1, source_target_pairs={{1,0},{2,1},{3,2},{0,3},{5,4},{6,5},{7,6},{4,7},{9,8},{10,9},{11,1... | collective-permute-start | bytes 98312 | tf_op jit(solution)/shard_map/ppermute | solution.py:32
  151.6 7.4 %shard_map.106 = (bf16[1024,128]{1,0:T(8,128)(2,1)S(1)}, f32[512,128]{1,0:T(8,128)S(1)}, f32[64,2048]{1,0:T(8,128)S(1)}) custom-call(s32[3]{0:T(128)S(1)} %add_add_fusion.meta, bf16[5120,2048]{1,0:T(8,128)(2,1)} %get-tuple-element.11.response_in.response, f32[2560,2048]{1,0:T(8,128)} %get-tuple-element.12.history_in), custom_call_target="tpu_custom_call" | custom-call | flops 1073741824 | bytes 12582912 | tf_op jit(solution)/shard_map/pallas_call | solution.py:264
  159.0 3.2 %shard_map.107 = f32[4,96,512]{2,1,0:T(8,128)S(1)} custom-call(s32[3]{0:T(128)S(1)} %add_add_fusion.meta, bf16[5120,2048]{1,0:T(8,128)(2,1)} %get-tuple-element.11.response_in.response, bf16[1024,128]{1,0:T(8,128)(2,1)S(1)} %get-tuple-element.13.at_ports, f32[512,128]{1,0:T(8,128)S(1)} %get-tuple-element.14.samples, f32[64,2048]{1,0:T(8,128)S(1)} %get-tuple-element.15.last, ...), custom_call_target="tpu_custom_call" | custom-call | flops 268435456 | bytes 12582912 | tf_op jit(solution)/shard_map/pallas_call | solution.py:264
  162.3 4.5 %collective-permute-start.22 = (f32[96,512]{1,0:T(8,128)S(1)}, f32[96,512]{1,0:T(8,128)S(1)}, u32[]{:S(2)}, u32[]{:S(2)}) collective-permute-start(f32[96,512]{1,0:T(8,128)S(1)} %get-tuple-element.18), channel_id=1, source_target_pairs={{0,1},{6,7},{8,9},{14,15},{16,17},{22,23},{24,25},{30,31},{32,33},... | collective-permute-start | bytes 589832 | tf_op jit(solution)/shard_map/ppermute | solution.py:21
  166.7 1.3 collective-permute-start.23
  168.0 1.3 collective-permute-start.24
  169.9 2.1 %collective-permute-done.23 = f32[96,512]{1,0:T(8,128)S(1)} collective-permute-done((f32[96,512]{1,0:T(8,128)S(1)}, f32[96,512]{1,0:T(8,128)S(1)}, u32[]{:S(2)}, u32[]{:S(2)}) %collective-permute-start.23) | collective-permute-done | bytes 196640 | tf_op jit(solution)/shard_map/ppermute | solution.py:21
  (79 shorter events, 22.9 us)
Async XLA Ops:
  0.7 39.0 %copy-start.6 = (bf16[1,32,512]{2,1,0:T(8,128)(2,1)S(1)}, bf16[1,32,512]{2,1,0:T(8,128)(2,1)}, u32[]{:S(2)}) copy-start(bf16[1,32,512]{2,1,0:T(8,128)(2,1)} %param.14) | copy-start | bytes 98308
  3.3 47.2 %collective-permute-start.1 = (bf16[1280,512]{1,0:T(8,128)(2,1)}, bf16[1280,512]{1,0:T(8,128)(2,1)}, u32[]{:S(2)}, u32[]{:S(2)}) collective-permute-start(bf16[1280,512]{1,0:T(8,128)(2,1)} %slice_bitcast_fusion), channel_id=1, source_target_pairs={{2,1},{4,7},{10,9},{12,15},{18,17},{20,23},{26,25},{28,31},{34,33}... | collective-permute-start | bytes 3932168 | tf_op jit(solution)/shard_map/ppermute | solution.py:21
  5.1 93.7 %collective-permute-start = (bf16[2048,512]{1,0:T(8,128)(2,1)S(1)}, bf16[2048,512]{1,0:T(8,128)(2,1)}, u32[]{:S(2)}, u32[]{:S(2)}) collective-permute-start(bf16[2048,512]{1,0:T(8,128)(2,1)S(1)} %bitcast.44), channel_id=1, source_target_pairs={{1,0},{7,6},{9,8},{15,14},{17,16},{23,22},{25,24},{31,30},{33,32},... | collective-permute-start | bytes 6291464 | tf_op jit(solution)/shard_map/ppermute | solution.py:21
  6.3 92.5 %collective-permute-start.5 = (bf16[2048,512]{1,0:T(8,128)(2,1)S(1)}, bf16[2048,512]{1,0:T(8,128)(2,1)}, u32[]{:S(2)}, u32[]{:S(2)}) collective-permute-start(bf16[2048,512]{1,0:T(8,128)(2,1)S(1)} %bitcast.45), channel_id=1, source_target_pairs={{3,0},{5,6},{11,8},{13,14},{19,16},{21,22},{27,24},{29,30},{35,32}... | collective-permute-start | bytes 6291464 | tf_op jit(solution)/shard_map/ppermute | solution.py:21
  8.0 9.4 %collective-permute-start.10 = (f32[8,512]{1,0:T(8,128)S(1)}, f32[8,512]{1,0:T(8,128)S(1)}, u32[]{:S(2)}, u32[]{:S(2)}) collective-permute-start(f32[8,512]{1,0:T(8,128)S(1)} %maximum_maximum_fusion.m0), channel_id=1, source_target_pairs={{2,0},{4,6},{10,8},{12,14},{18,16},{20,22},{26,24},{28,30},{34,32}... | collective-permute-start | bytes 49160 | tf_op jit(solution)/shard_map/ppermute | solution.py:21
  9.3 26.6 %collective-permute-start.11 = (f32[8,512]{1,0:T(8,128)S(1)}, f32[8,512]{1,0:T(8,128)S(1)}, u32[]{:S(2)}, u32[]{:S(2)}) collective-permute-start(f32[8,512]{1,0:T(8,128)S(1)} %maximum_maximum_fusion.m0), channel_id=1, source_target_pairs={{3,0},{5,6},{11,8},{13,14},{19,16},{21,22},{27,24},{29,30},{35,32}... | collective-permute-start | bytes 49160 | tf_op jit(solution)/shard_map/ppermute | solution.py:21
  11.4 54.0 %copy-start.8 = (s32[32]{0:T(128)S(1)}, s32[32]{0:T(128)}, u32[]{:S(2)}) copy-start(s32[32]{0:T(128)} %param.17) | copy-start | bytes 388
  11.4 54.0 %copy-start.10 = (s32[1,32]{1,0:T(1,128)S(1)}, s32[1,32]{1,0:T(1,128)}, u32[]{:S(2)}) copy-start(s32[1,32]{1,0:T(1,128)} %param.16) | copy-start | bytes 388
  11.4 55.0 %copy-start.3 = (f32[1,64,512]{2,1,0:T(8,128)S(1)}, f32[1,64,512]{2,1,0:T(8,128)}, u32[]{:S(2)}) copy-start(f32[1,64,512]{2,1,0:T(8,128)} %param.9) | copy-start | bytes 393220
  17.4 20.6 %collective-permute-start.9 = (f32[8,512]{1,0:T(8,128)S(1)}, f32[8,512]{1,0:T(8,128)S(1)}, u32[]{:S(2)}, u32[]{:S(2)}) collective-permute-start(f32[8,512]{1,0:T(8,128)S(1)} %maximum_maximum_fusion.m0), channel_id=1, source_target_pairs={{1,0},{7,6},{9,8},{15,14},{17,16},{23,22},{25,24},{31,30},{33,32},... | collective-permute-start | bytes 49160 | tf_op jit(solution)/shard_map/ppermute | solution.py:21
  35.8 13.4 %collective-permute-start.6 = (bf16[7,64,512]{2,1,0:T(8,128)(2,1)}, bf16[7,64,512]{2,1,0:T(8,128)(2,1)}, u32[]{:S(2)}, u32[]{:S(2)}) collective-permute-start(bf16[7,64,512]{2,1,0:T(8,128)(2,1)} %slice_bitcast_fusion.2.s0_in), channel_id=1, source_target_pairs={{1,0},{7,6},{9,8},{15,14},{17,16},{23,22},{25,24},{31,30},{33,32},... | collective-permute-start | bytes 1376264 | tf_op jit(solution)/shard_map/ppermute | solution.py:21
  38.1 25.3 %collective-permute-start.3 = (bf16[768,512]{1,0:T(8,128)(2,1)}, bf16[768,512]{1,0:T(8,128)(2,1)}, u32[]{:S(2)}, u32[]{:S(2)}) collective-permute-start(bf16[768,512]{1,0:T(8,128)(2,1)} %slice_bitcast_fusion.1), channel_id=1, source_target_pairs={{2,3},{4,5},{10,11},{12,13},{18,19},{20,21},{26,27},{28,29},{34,35... | collective-permute-start | bytes 2359304 | tf_op jit(solution)/shard_map/ppermute | solution.py:21
  40.7 25.7 %all-to-all-start = ((bf16[32,32,512]{2,1,0:T(8,128)(2,1)}), bf16[32,32,512]{2,1,0:T(8,128)(2,1)S(1)}, u32[]{:S(2)}, u32[]{:S(2)}) async-start(bf16[32,32,512]{2,1,0:T(8,128)(2,1)} %broadcast_in_dim.97), calls=%async_computation | async-start | bytes 2097152 | tf_op jit(solution)/shard_map/all_to_all | solution.py:287
  49.2 12.1 %collective-permute-start.7 = (bf16[7,64,512]{2,1,0:T(8,128)(2,1)}, bf16[7,64,512]{2,1,0:T(8,128)(2,1)S(1)}, u32[]{:S(2)}, u32[]{:S(2)}) collective-permute-start(bf16[7,64,512]{2,1,0:T(8,128)(2,1)} %slice_bitcast_fusion.2.s0_in), channel_id=1, source_target_pairs={{2,0},{4,6},{10,8},{12,14},{18,16},{20,22},{26,24},{28,30},{34,32}... | collective-permute-start | bytes 1376264 | tf_op jit(solution)/shard_map/ppermute | solution.py:21
  50.5 48.3 %collective-permute-start.2 = (bf16[1280,512]{1,0:T(8,128)(2,1)}, bf16[1280,512]{1,0:T(8,128)(2,1)}, u32[]{:S(2)}, u32[]{:S(2)}) collective-permute-start(bf16[1280,512]{1,0:T(8,128)(2,1)} %collective-permute-done.1), channel_id=1, source_target_pairs={{1,0},{7,6},{9,8},{15,14},{17,16},{23,22},{25,24},{31,30},{33,32},... | collective-permute-start | bytes 3932168 | tf_op jit(solution)/shard_map/ppermute | solution.py:21
  62.1 11.9 %collective-permute-start.8 = (bf16[7,64,512]{2,1,0:T(8,128)(2,1)}, bf16[7,64,512]{2,1,0:T(8,128)(2,1)}, u32[]{:S(2)}, u32[]{:S(2)}) collective-permute-start(bf16[7,64,512]{2,1,0:T(8,128)(2,1)} %slice_bitcast_fusion.2.s0_in), channel_id=1, source_target_pairs={{3,0},{5,6},{11,8},{13,14},{19,16},{21,22},{27,24},{29,30},{35,32}... | collective-permute-start | bytes 1376264 | tf_op jit(solution)/shard_map/ppermute | solution.py:21
  63.4 35.4 %collective-permute-start.4 = (bf16[768,512]{1,0:T(8,128)(2,1)}, bf16[768,512]{1,0:T(8,128)(2,1)}, u32[]{:S(2)}, u32[]{:S(2)}) collective-permute-start(bf16[768,512]{1,0:T(8,128)(2,1)} %collective-permute-done.3), channel_id=1, source_target_pairs={{3,0},{5,6},{11,8},{13,14},{19,16},{21,22},{27,24},{29,30},{35,32}... | collective-permute-start | bytes 2359304 | tf_op jit(solution)/shard_map/ppermute | solution.py:21
  74.0 9.1 %collective-permute-start.12 = (bf16[96,512]{1,0:T(8,128)(2,1)S(1)}, bf16[96,512]{1,0:T(8,128)(2,1)S(1)}, u32[]{:S(2)}, u32[]{:S(2)}) collective-permute-start(bf16[96,512]{1,0:T(8,128)(2,1)S(1)} %get-tuple-element.10.w0), channel_id=1, source_target_pairs={{1,0},{7,6},{9,8},{15,14},{17,16},{23,22},{25,24},{31,30},{33,32},... | collective-permute-start | bytes 294920 | tf_op jit(solution)/shard_map/ppermute | solution.py:21
  75.9 16.4 %all-to-all-start.1 = ((bf16[16,16,128]{2,1,0:T(8,128)(2,1)}), bf16[16,16,128]{2,1,0:T(8,128)(2,1)S(1)}, u32[]{:S(2)}, u32[]{:S(2)}) async-start(bf16[16,16,128]{2,1,0:T(8,128)(2,1)} %broadcast_in_dim.98), calls=%async_computation.1 | async-start | bytes 131072 | tf_op jit(solution)/shard_map/all_to_all | solution.py:316
  83.1 8.0 %collective-permute-start.13 = (bf16[96,512]{1,0:T(8,128)(2,1)S(1)}, bf16[96,512]{1,0:T(8,128)(2,1)S(1)}, u32[]{:S(2)}, u32[]{:S(2)}) collective-permute-start(bf16[96,512]{1,0:T(8,128)(2,1)S(1)} %get-tuple-element.10.w0), channel_id=1, source_target_pairs={{2,0},{4,6},{10,8},{12,14},{18,16},{20,22},{26,24},{28,30},{34,32}... | collective-permute-start | bytes 294920 | tf_op jit(solution)/shard_map/ppermute | solution.py:21
  91.1 7.7 %collective-permute-start.14 = (bf16[96,512]{1,0:T(8,128)(2,1)S(1)}, bf16[96,512]{1,0:T(8,128)(2,1)S(1)}, u32[]{:S(2)}, u32[]{:S(2)}) collective-permute-start(bf16[96,512]{1,0:T(8,128)(2,1)S(1)} %get-tuple-element.10.w0), channel_id=1, source_target_pairs={{3,0},{5,6},{11,8},{13,14},{19,16},{21,22},{27,24},{29,30},{35,32}... | collective-permute-start | bytes 294920 | tf_op jit(solution)/shard_map/ppermute | solution.py:21
  121.9 4.4 %collective-permute-start.15 = (bf16[32,512]{1,0:T(8,128)(2,1)S(1)}, bf16[32,512]{1,0:T(8,128)(2,1)S(1)}, u32[]{:S(2)}, u32[]{:S(2)}) collective-permute-start(bf16[32,512]{1,0:T(8,128)(2,1)S(1)} %get-tuple-element.23), channel_id=1, source_target_pairs={{0,1},{6,7},{8,9},{14,15},{16,17},{22,23},{24,25},{30,31},{32,33},... | collective-permute-start | bytes 98312 | tf_op jit(solution)/shard_map/ppermute | solution.py:21
  123.2 3.1 %collective-permute-start.16 = (bf16[32,512]{1,0:T(8,128)(2,1)S(1)}, bf16[32,512]{1,0:T(8,128)(2,1)S(1)}, u32[]{:S(2)}, u32[]{:S(2)}) collective-permute-start(bf16[32,512]{1,0:T(8,128)(2,1)S(1)} %get-tuple-element.22), channel_id=1, source_target_pairs={{0,2},{6,4},{8,10},{14,12},{16,18},{22,20},{24,26},{30,28},{32,34}... | collective-permute-start | bytes 98312 | tf_op jit(solution)/shard_map/ppermute | solution.py:21
  124.5 2.9 %collective-permute-start.17 = (bf16[32,512]{1,0:T(8,128)(2,1)S(1)}, bf16[32,512]{1,0:T(8,128)(2,1)S(1)}, u32[]{:S(2)}, u32[]{:S(2)}) collective-permute-start(bf16[32,512]{1,0:T(8,128)(2,1)S(1)} %get-tuple-element.21), channel_id=1, source_target_pairs={{0,3},{6,5},{8,11},{14,13},{16,19},{22,21},{24,27},{30,29},{32,35}... | collective-permute-start | bytes 98312 | tf_op jit(solution)/shard_map/ppermute | solution.py:21
  127.4 1.3 collective-permute-start.18
  129.7 17.2 %all-to-all-start.2 = ((bf16[16,32,512]{2,1,0:T(8,128)(2,1)}), bf16[16,32,512]{2,1,0:T(8,128)(2,1)S(1)}, u32[]{:S(2)}, u32[]{:S(2)}) async-start(bf16[16,32,512]{2,1,0:T(8,128)(2,1)} %select_select_fusion), calls=%async_computation.2 | async-start | bytes 1048576 | tf_op jit(solution)/shard_map/all_to_all | solution.py:332
  147.1 11.9 %collective-permute-start.19 = (bf16[32,512]{1,0:T(8,128)(2,1)S(1)}, bf16[32,512]{1,0:T(8,128)(2,1)S(1)}, u32[]{:S(2)}, u32[]{:S(2)}) collective-permute-start(bf16[32,512]{1,0:T(8,128)(2,1)S(1)} %multiply_convert_fusion.v0), channel_id=1, source_target_pairs={{1,0},{2,1},{3,2},{0,3},{5,4},{6,5},{7,6},{4,7},{9,8},{10,9},{11,1... | collective-permute-start | bytes 98312 | tf_op jit(solution)/shard_map/ppermute | solution.py:32
  150.6 8.3 %collective-permute-start.20 = (bf16[32,512]{1,0:T(8,128)(2,1)S(1)}, bf16[32,512]{1,0:T(8,128)(2,1)S(1)}, u32[]{:S(2)}, u32[]{:S(2)}) collective-permute-start(bf16[32,512]{1,0:T(8,128)(2,1)S(1)} %multiply_convert_fusion.v0), channel_id=1, source_target_pairs={{2,0},{3,1},{0,2},{1,3},{6,4},{7,5},{4,6},{5,7},{10,8},{11,9},{8,1... | collective-permute-start | bytes 98312 | tf_op jit(solution)/shard_map/ppermute | solution.py:32
  150.6 8.3 %collective-permute-start.21 = (bf16[32,512]{1,0:T(8,128)(2,1)S(1)}, bf16[32,512]{1,0:T(8,128)(2,1)S(1)}, u32[]{:S(2)}, u32[]{:S(2)}) collective-permute-start(bf16[32,512]{1,0:T(8,128)(2,1)S(1)} %multiply_convert_fusion.v0), channel_id=1, source_target_pairs={{3,0},{0,1},{1,2},{2,3},{7,4},{4,5},{5,6},{6,7},{11,8},{8,9},{9,10... | collective-permute-start | bytes 98312 | tf_op jit(solution)/shard_map/ppermute | solution.py:32
  162.3 7.6 %collective-permute-start.22 = (f32[96,512]{1,0:T(8,128)S(1)}, f32[96,512]{1,0:T(8,128)S(1)}, u32[]{:S(2)}, u32[]{:S(2)}) collective-permute-start(f32[96,512]{1,0:T(8,128)S(1)} %get-tuple-element.18), channel_id=1, source_target_pairs={{0,1},{6,7},{8,9},{14,15},{16,17},{22,23},{24,25},{30,31},{32,33},... | collective-permute-start | bytes 589832 | tf_op jit(solution)/shard_map/ppermute | solution.py:21
  166.7 5.3 %collective-permute-start.23 = (f32[96,512]{1,0:T(8,128)S(1)}, f32[96,512]{1,0:T(8,128)S(1)}, u32[]{:S(2)}, u32[]{:S(2)}) collective-permute-start(f32[96,512]{1,0:T(8,128)S(1)} %get-tuple-element.20), channel_id=1, source_target_pairs={{0,2},{6,4},{8,10},{14,12},{16,18},{22,20},{24,26},{30,28},{32,34}... | collective-permute-start | bytes 589832 | tf_op jit(solution)/shard_map/ppermute | solution.py:21
  168.0 4.5 %collective-permute-start.24 = (f32[96,512]{1,0:T(8,128)S(1)}, f32[96,512]{1,0:T(8,128)S(1)}, u32[]{:S(2)}, u32[]{:S(2)}) collective-permute-start(f32[96,512]{1,0:T(8,128)S(1)} %get-tuple-element.19), channel_id=1, source_target_pairs={{0,3},{6,5},{8,11},{14,13},{16,19},{22,21},{24,27},{30,29},{32,35}... | collective-permute-start | bytes 589832 | tf_op jit(solution)/shard_map/ppermute | solution.py:21
  (7 other events, 31.5 us)

commit v3 on v2

--- a/solution.py
+++ b/solution.py
@@ -258,6 +258,22 @@
         out[d, cases:, :] = wave[d * ports : (d + 1) * ports]
 
 
+def choose_kernel(rel, home, one, two, three, last, waveform, sent):
+    cases, rows = last.shape[0], one.shape[0]
+    for d, part in enumerate((home.at[0], one, two, three)):
+
+        @pl.when(rel[0] == d)
+        def _(part=part):
+            copies = (
+                pltpu.make_async_copy(part.at[pl.ds(0, cases), :], last, sent.at[0]),
+                pltpu.make_async_copy(part.at[pl.ds(cases, rows - cases), :], waveform, sent.at[1]),
+            )
+            for copy in copies:
+                copy.start()
+            for copy in copies:
+                copy.wait()
+
+
 def call(kernel, outs, scratch, flops, limit, meta, *operands, hbm_outs=(), hbm_ins=()):
     vmem, hbm = pl.BlockSpec(memory_space=pltpu.VMEM), pl.BlockSpec(memory_space=pltpu.HBM)
     outs = tuple(outs)
@@ -407,9 +423,13 @@
         2 * cases * steps * all_ports * nodes, LIMITS[2], meta,
         response, at_ports, samples, last, *drives, hbm_ins=(0,),
     )
-    parts = from_home(result)
-    last = mine(parts, rel, slice(0, cases))
-    waveform = mine(parts, rel, slice(cases, None))
+    parts = (result, *from_home(result)[1:])
+    last, waveform = call(
+        choose_kernel,
+        (shape((cases, block), F32), shape((ports, steps * cases), F32)),
+        [pltpu.SemaphoreType.DMA((2,))], 1 << 20, 8, rel.astype(jnp.int32)[None], *parts,
+        hbm_outs=(0, 1),
+    )
     return last[None], waveform[None]
 
 

time: 176 us -> 175 us (level)
    pallas_call x4 -> x5, Pallas kernels: 33.7 us -> 34.4 us  [call(): pl.pallas_call(kernel, out_shape=outs, in_specs=[pl.BlockSpec(memory_spac...]
where the time goes in v3:
time: 175 us; the launch traced here: 173 us
  waiting for transfers between devices  69.1 us (39%)
  starting transfers between devices  56.5 us (32%)
  Pallas kernels  34.4 us (20%)
  local copies, waits for them, and re-layouts  9.43 us (5%)
  other arithmetic  2.07 us (1%)
  between operations  1.94 us (1%)
    ppermute x21, waiting for transfers between devices, hop(): return lax.ppermute(array, ('sub', 'blk'), pairs)  55.3 us
    pallas_call x5, Pallas kernels, call(): pl.pallas_call(kernel, out_shape=outs, in_specs=[pl.BlockSpec(memory_spac...  34.4 us
    ppermute x21, starting transfers between devices, hop(): return lax.ppermute(array, ('sub', 'blk'), pairs)  30.9 us
    all_to_all x1, waiting for transfers between devices, second_fetch(): lax.all_to_all(sent, 'sub', split_axis=0, concat_axis=0, axis_index_group...  11.8 us
    all_to_all x1, starting transfers between devices, first_exchange(): lax.all_to_all(copies, 'sub', split_axis=0, concat_axis=0, tiled=True)  8.45 us
    all_to_all x1, starting transfers between devices, requests(): lax.all_to_all(copies, 'sub', split_axis=0, concat_axis=0, axis_index_gro...  7.1 us
    all_to_all x1, starting transfers between devices, second_fetch(): lax.all_to_all(sent, 'sub', split_axis=0, concat_axis=0, axis_index_group...  5.41 us
    ppermute x3, starting transfers between devices, turn(): parts.append(lax.ppermute(array, ('sub', 'blk'), pairs))  4.49 us
  transfers between devices with their start and end apart: 28, of which 13 were waited for; matrix products, arithmetic and copies ran while one was open for 3% of the time, Pallas kernels for 5%

profile of v3, /device:TPU:0, one launch (start us, length us, event | category | flops | bytes accessed | tf_op | source)
XLA Modules:
  0.0 173.4 jit_solution(7828509123714176962)
XLA Ops:
  0.7 2.6 %slice_bitcast_fusion = bf16[1280,512]{1,0:T(8,128)(2,1)} fusion(bf16[1,2048,512]{2,1,0:T(8,128)(2,1)} %param.12), kind=kLoop, calls=%fused_computation | loop fusion | bytes 2621440 | tf_op jit(solution)/shard_map/slice | solution.py:48
  3.3 1.7 %collective-permute-start.1 = (bf16[1280,512]{1,0:T(8,128)(2,1)}, bf16[1280,512]{1,0:T(8,128)(2,1)}, u32[]{:S(2)}, u32[]{:S(2)}) collective-permute-start(bf16[1280,512]{1,0:T(8,128)(2,1)} %slice_bitcast_fusion), channel_id=1, source_target_pairs={{2,1},{4,7},{10,9},{12,15},{18,17},{20,23},{26,25},{28,31},{34,33}... | collective-permute-start | bytes 3932168 | tf_op jit(solution)/shard_map/ppermute | solution.py:21
  5.0 1.3 collective-permute-start
  6.3 1.3 collective-permute-start.5
  8.0 1.3 collective-permute-start.10
  9.3 1.3 collective-permute-start.11
  11.4 6.0 %collective-permute-done.10.m2 = f32[8,512]{1,0:T(8,128)S(1)} collective-permute-done((f32[8,512]{1,0:T(8,128)S(1)}, f32[8,512]{1,0:T(8,128)S(1)}, u32[]{:S(2)}, u32[]{:S(2)}) %collective-permute-start.10) | collective-permute-done | bytes 16416 | tf_op jit(solution)/shard_map/ppermute | solution.py:21
  18.7 17.1 %collective-permute-done.11.m3 = f32[8,512]{1,0:T(8,128)S(1)} collective-permute-done((f32[8,512]{1,0:T(8,128)S(1)}, f32[8,512]{1,0:T(8,128)S(1)}, u32[]{:S(2)}, u32[]{:S(2)}) %collective-permute-start.11) | collective-permute-done | bytes 16416 | tf_op jit(solution)/shard_map/ppermute | solution.py:21
  38.1 1.5 collective-permute-start.3
  40.7 8.4 %all-to-all-start = ((bf16[32,32,512]{2,1,0:T(8,128)(2,1)}), bf16[32,32,512]{2,1,0:T(8,128)(2,1)S(1)}, u32[]{:S(2)}, u32[]{:S(2)}) async-start(bf16[32,32,512]{2,1,0:T(8,128)(2,1)} %broadcast_in_dim.101), calls=%async_computation | async-start | bytes 2097152 | tf_op jit(solution)/shard_map/all_to_all | solution.py:303
  49.2 1.3 collective-permute-start.7
  50.5 1.3 collective-permute-start.2
  51.8 9.5 %collective-permute-done.7.s2_in = bf16[7,64,512]{2,1,0:T(8,128)(2,1)S(1)} collective-permute-done((bf16[7,64,512]{2,1,0:T(8,128)(2,1)}, bf16[7,64,512]{2,1,0:T(8,128)(2,1)S(1)}, u32[]{:S(2)}, u32[]{:S(2)}) %collective-permute-start.7) | collective-permute-done | bytes 458784 | tf_op jit(solution)/shard_map/ppermute | solution.py:21
  63.4 1.3 collective-permute-start.4
  68.6 5.4 %collective-permute-done.8.s3_in = bf16[7,64,512]{2,1,0:T(8,128)(2,1)} collective-permute-done((bf16[7,64,512]{2,1,0:T(8,128)(2,1)}, bf16[7,64,512]{2,1,0:T(8,128)(2,1)}, u32[]{:S(2)}, u32[]{:S(2)}) %collective-permute-start.8) | collective-permute-done | bytes 458784 | tf_op jit(solution)/shard_map/ppermute | solution.py:21
  75.9 7.1 %all-to-all-start.1 = ((bf16[16,16,128]{2,1,0:T(8,128)(2,1)}), bf16[16,16,128]{2,1,0:T(8,128)(2,1)S(1)}, u32[]{:S(2)}, u32[]{:S(2)}) async-start(bf16[16,16,128]{2,1,0:T(8,128)(2,1)} %broadcast_in_dim.102), calls=%async_computation.1 | async-start | bytes 131072 | tf_op jit(solution)/shard_map/all_to_all | solution.py:332
  83.1 1.3 collective-permute-start.13
  84.4 6.6 %collective-permute-done.13.w2 = bf16[96,512]{1,0:T(8,128)(2,1)S(1)} collective-permute-done((bf16[96,512]{1,0:T(8,128)(2,1)S(1)}, bf16[96,512]{1,0:T(8,128)(2,1)S(1)}, u32[]{:S(2)}, u32[]{:S(2)}) %collective-permute-start.13) | collective-permute-done | bytes 98336 | tf_op jit(solution)/shard_map/ppermute | solution.py:21
  92.4 6.4 %collective-permute-done.14.w3 = bf16[96,512]{1,0:T(8,128)(2,1)S(1)} collective-permute-done((bf16[96,512]{1,0:T(8,128)(2,1)S(1)}, bf16[96,512]{1,0:T(8,128)(2,1)S(1)}, u32[]{:S(2)}, u32[]{:S(2)}) %collective-permute-start.14) | collective-permute-done | bytes 98336 | tf_op jit(solution)/shard_map/ppermute | solution.py:21
  99.8 22.0 %shard_map.105 = (bf16[4,32,512]{2,1,0:T(8,128)(2,1)S(1)}, bf16[5120,2048]{1,0:T(8,128)(2,1)}, f32[2560,2048]{1,0:T(8,128)}) custom-call(s32[3]{0:T(128)S(1)} %add_add_fusion.1.meta, bf16[2048,512]{1,0:T(8,128)(2,1)S(1)} %bitcast.37, bf16[2048,512]{1,0:T(8,128)(2,1)} %collective-permute-done.a1_in, bf16[1280,512]{1,0:T(8,128)(2,1)} %collective-permute-done.2.a2_in, ...), custom_call_target="tpu_custom_call" | custom-call | flops 12884901888 | bytes 12582912 | tf_op jit(solution)/shard_map/pallas_call | solution.py:280
  121.9 1.3 collective-permute-start.15
  123.2 1.3 collective-permute-start.16
  124.5 1.3 collective-permute-start.17
  129.7 5.4 %all-to-all-start.2 = ((bf16[16,32,512]{2,1,0:T(8,128)(2,1)}), bf16[16,32,512]{2,1,0:T(8,128)(2,1)S(1)}, u32[]{:S(2)}, u32[]{:S(2)}) async-start(bf16[16,32,512]{2,1,0:T(8,128)(2,1)} %select_select_fusion), calls=%async_computation.2 | async-start | bytes 1048576 | tf_op jit(solution)/shard_map/all_to_all | solution.py:348
  135.1 11.8 %all-to-all-done.2 = bf16[16,32,512]{2,1,0:T(8,128)(2,1)S(1)} async-done(((bf16[16,32,512]{2,1,0:T(8,128)(2,1)}), bf16[16,32,512]{2,1,0:T(8,128)(2,1)S(1)}, u32[]{:S(2)}, u32[]{:S(2)}) %all-to-all-start.2) | async-done | bytes 524320 | tf_op jit(solution)/shard_map/all_to_all | solution.py:348
  147.1 3.5 %collective-permute-start.19 = (bf16[32,512]{1,0:T(8,128)(2,1)S(1)}, bf16[32,512]{1,0:T(8,128)(2,1)S(1)}, u32[]{:S(2)}, u32[]{:S(2)}) collective-permute-start(bf16[32,512]{1,0:T(8,128)(2,1)S(1)} %multiply_convert_fusion.v0), channel_id=1, source_target_pairs={{1,0},{2,1},{3,2},{0,3},{5,4},{6,5},{7,6},{4,7},{9,8},{10,9},{11,1... | collective-permute-start | bytes 98312 | tf_op jit(solution)/shard_map/ppermute | solution.py:32
  151.6 7.4 %shard_map.106 = (bf16[1024,128]{1,0:T(8,128)(2,1)S(1)}, f32[512,128]{1,0:T(8,128)S(1)}, f32[64,2048]{1,0:T(8,128)S(1)}) custom-call(s32[3]{0:T(128)S(1)} %add_add_fusion.meta, bf16[5120,2048]{1,0:T(8,128)(2,1)} %get-tuple-element.13.response_in.response, f32[2560,2048]{1,0:T(8,128)} %get-tuple-element.14.history_in), custom_call_target="tpu_custom_call" | custom-call | flops 1073741824 | bytes 12582912 | tf_op jit(solution)/shard_map/pallas_call | solution.py:280
  159.0 3.2 %shard_map.107.home = f32[4,96,512]{2,1,0:T(8,128)S(1)} custom-call(s32[3]{0:T(128)S(1)} %add_add_fusion.meta, bf16[5120,2048]{1,0:T(8,128)(2,1)} %get-tuple-element.13.response_in.response, bf16[1024,128]{1,0:T(8,128)(2,1)S(1)} %get-tuple-element.15.at_ports, f32[512,128]{1,0:T(8,128)S(1)} %get-tuple-element.16.samples, ...), custom_call_target="tpu_custom_call" | custom-call | flops 268435456 | bytes 12582912 | tf_op jit(solution)/shard_map/pallas_call | solution.py:280
  162.3 4.5 %collective-permute-start.22 = (f32[96,512]{1,0:T(8,128)S(1)}, f32[96,512]{1,0:T(8,128)S(1)}, u32[]{:S(2)}, u32[]{:S(2)}) collective-permute-start(f32[96,512]{1,0:T(8,128)S(1)} %get-tuple-element.24), channel_id=1, source_target_pairs={{0,1},{6,7},{8,9},{14,15},{16,17},{22,23},{24,25},{30,31},{32,33},... | collective-permute-start | bytes 589832 | tf_op jit(solution)/shard_map/ppermute | solution.py:21
  166.7 1.3 collective-permute-start.23
  168.1 1.3 collective-permute-start.24
  169.9 2.1 %collective-permute-done.23.two = f32[96,512]{1,0:T(8,128)S(1)} collective-permute-done((f32[96,512]{1,0:T(8,128)S(1)}, f32[96,512]{1,0:T(8,128)S(1)}, u32[]{:S(2)}, u32[]{:S(2)}) %collective-permute-start.23) | collective-permute-done | bytes 196640 | tf_op jit(solution)/shard_map/ppermute | solution.py:21
  (78 shorter events, 22.2 us)
Async XLA Ops:
  0.7 39.0 %copy-start.6 = (bf16[1,32,512]{2,1,0:T(8,128)(2,1)S(1)}, bf16[1,32,512]{2,1,0:T(8,128)(2,1)}, u32[]{:S(2)}) copy-start(bf16[1,32,512]{2,1,0:T(8,128)(2,1)} %param.14) | copy-start | bytes 98308
  3.3 47.2 %collective-permute-start.1 = (bf16[1280,512]{1,0:T(8,128)(2,1)}, bf16[1280,512]{1,0:T(8,128)(2,1)}, u32[]{:S(2)}, u32[]{:S(2)}) collective-permute-start(bf16[1280,512]{1,0:T(8,128)(2,1)} %slice_bitcast_fusion), channel_id=1, source_target_pairs={{2,1},{4,7},{10,9},{12,15},{18,17},{20,23},{26,25},{28,31},{34,33}... | collective-permute-start | bytes 3932168 | tf_op jit(solution)/shard_map/ppermute | solution.py:21
  5.0 93.7 %collective-permute-start = (bf16[2048,512]{1,0:T(8,128)(2,1)S(1)}, bf16[2048,512]{1,0:T(8,128)(2,1)}, u32[]{:S(2)}, u32[]{:S(2)}) collective-permute-start(bf16[2048,512]{1,0:T(8,128)(2,1)S(1)} %bitcast.35), channel_id=1, source_target_pairs={{1,0},{7,6},{9,8},{15,14},{17,16},{23,22},{25,24},{31,30},{33,32},... | collective-permute-start | bytes 6291464 | tf_op jit(solution)/shard_map/ppermute | solution.py:21
  6.3 92.5 %collective-permute-start.5 = (bf16[2048,512]{1,0:T(8,128)(2,1)S(1)}, bf16[2048,512]{1,0:T(8,128)(2,1)}, u32[]{:S(2)}, u32[]{:S(2)}) collective-permute-start(bf16[2048,512]{1,0:T(8,128)(2,1)S(1)} %bitcast.36), channel_id=1, source_target_pairs={{3,0},{5,6},{11,8},{13,14},{19,16},{21,22},{27,24},{29,30},{35,32}... | collective-permute-start | bytes 6291464 | tf_op jit(solution)/shard_map/ppermute | solution.py:21
  8.0 9.4 %collective-permute-start.10 = (f32[8,512]{1,0:T(8,128)S(1)}, f32[8,512]{1,0:T(8,128)S(1)}, u32[]{:S(2)}, u32[]{:S(2)}) collective-permute-start(f32[8,512]{1,0:T(8,128)S(1)} %maximum_maximum_fusion.m0), channel_id=1, source_target_pairs={{2,0},{4,6},{10,8},{12,14},{18,16},{20,22},{26,24},{28,30},{34,32}... | collective-permute-start | bytes 49160 | tf_op jit(solution)/shard_map/ppermute | solution.py:21
  9.3 26.6 %collective-permute-start.11 = (f32[8,512]{1,0:T(8,128)S(1)}, f32[8,512]{1,0:T(8,128)S(1)}, u32[]{:S(2)}, u32[]{:S(2)}) collective-permute-start(f32[8,512]{1,0:T(8,128)S(1)} %maximum_maximum_fusion.m0), channel_id=1, source_target_pairs={{3,0},{5,6},{11,8},{13,14},{19,16},{21,22},{27,24},{29,30},{35,32}... | collective-permute-start | bytes 49160 | tf_op jit(solution)/shard_map/ppermute | solution.py:21
  11.4 54.0 %copy-start.8 = (s32[32]{0:T(128)S(1)}, s32[32]{0:T(128)}, u32[]{:S(2)}) copy-start(s32[32]{0:T(128)} %param.17) | copy-start | bytes 388
  11.4 54.0 %copy-start.10 = (s32[1,32]{1,0:T(1,128)S(1)}, s32[1,32]{1,0:T(1,128)}, u32[]{:S(2)}) copy-start(s32[1,32]{1,0:T(1,128)} %param.16) | copy-start | bytes 388
  11.4 55.0 %copy-start.3 = (f32[1,64,512]{2,1,0:T(8,128)S(1)}, f32[1,64,512]{2,1,0:T(8,128)}, u32[]{:S(2)}) copy-start(f32[1,64,512]{2,1,0:T(8,128)} %param.9) | copy-start | bytes 393220
  17.4 20.6 %collective-permute-start.9 = (f32[8,512]{1,0:T(8,128)S(1)}, f32[8,512]{1,0:T(8,128)S(1)}, u32[]{:S(2)}, u32[]{:S(2)}) collective-permute-start(f32[8,512]{1,0:T(8,128)S(1)} %maximum_maximum_fusion.m0), channel_id=1, source_target_pairs={{1,0},{7,6},{9,8},{15,14},{17,16},{23,22},{25,24},{31,30},{33,32},... | collective-permute-start | bytes 49160 | tf_op jit(solution)/shard_map/ppermute | solution.py:21
  35.8 13.4 %collective-permute-start.6 = (bf16[7,64,512]{2,1,0:T(8,128)(2,1)}, bf16[7,64,512]{2,1,0:T(8,128)(2,1)}, u32[]{:S(2)}, u32[]{:S(2)}) collective-permute-start(bf16[7,64,512]{2,1,0:T(8,128)(2,1)} %slice_bitcast_fusion.2.s0_in), channel_id=1, source_target_pairs={{1,0},{7,6},{9,8},{15,14},{17,16},{23,22},{25,24},{31,30},{33,32},... | collective-permute-start | bytes 1376264 | tf_op jit(solution)/shard_map/ppermute | solution.py:21
  38.1 25.3 %collective-permute-start.3 = (bf16[768,512]{1,0:T(8,128)(2,1)}, bf16[768,512]{1,0:T(8,128)(2,1)}, u32[]{:S(2)}, u32[]{:S(2)}) collective-permute-start(bf16[768,512]{1,0:T(8,128)(2,1)} %slice_bitcast_fusion.1), channel_id=1, source_target_pairs={{2,3},{4,5},{10,11},{12,13},{18,19},{20,21},{26,27},{28,29},{34,35... | collective-permute-start | bytes 2359304 | tf_op jit(solution)/shard_map/ppermute | solution.py:21
  40.7 25.7 %all-to-all-start = ((bf16[32,32,512]{2,1,0:T(8,128)(2,1)}), bf16[32,32,512]{2,1,0:T(8,128)(2,1)S(1)}, u32[]{:S(2)}, u32[]{:S(2)}) async-start(bf16[32,32,512]{2,1,0:T(8,128)(2,1)} %broadcast_in_dim.101), calls=%async_computation | async-start | bytes 2097152 | tf_op jit(solution)/shard_map/all_to_all | solution.py:303
  49.2 12.1 %collective-permute-start.7 = (bf16[7,64,512]{2,1,0:T(8,128)(2,1)}, bf16[7,64,512]{2,1,0:T(8,128)(2,1)S(1)}, u32[]{:S(2)}, u32[]{:S(2)}) collective-permute-start(bf16[7,64,512]{2,1,0:T(8,128)(2,1)} %slice_bitcast_fusion.2.s0_in), channel_id=1, source_target_pairs={{2,0},{4,6},{10,8},{12,14},{18,16},{20,22},{26,24},{28,30},{34,32}... | collective-permute-start | bytes 1376264 | tf_op jit(solution)/shard_map/ppermute | solution.py:21
  50.5 48.3 %collective-permute-start.2 = (bf16[1280,512]{1,0:T(8,128)(2,1)}, bf16[1280,512]{1,0:T(8,128)(2,1)}, u32[]{:S(2)}, u32[]{:S(2)}) collective-permute-start(bf16[1280,512]{1,0:T(8,128)(2,1)} %collective-permute-done.1), channel_id=1, source_target_pairs={{1,0},{7,6},{9,8},{15,14},{17,16},{23,22},{25,24},{31,30},{33,32},... | collective-permute-start | bytes 3932168 | tf_op jit(solution)/shard_map/ppermute | solution.py:21
  62.1 11.9 %collective-permute-start.8 = (bf16[7,64,512]{2,1,0:T(8,128)(2,1)}, bf16[7,64,512]{2,1,0:T(8,128)(2,1)}, u32[]{:S(2)}, u32[]{:S(2)}) collective-permute-start(bf16[7,64,512]{2,1,0:T(8,128)(2,1)} %slice_bitcast_fusion.2.s0_in), channel_id=1, source_target_pairs={{3,0},{5,6},{11,8},{13,14},{19,16},{21,22},{27,24},{29,30},{35,32}... | collective-permute-start | bytes 1376264 | tf_op jit(solution)/shard_map/ppermute | solution.py:21
  63.4 35.4 %collective-permute-start.4 = (bf16[768,512]{1,0:T(8,128)(2,1)}, bf16[768,512]{1,0:T(8,128)(2,1)}, u32[]{:S(2)}, u32[]{:S(2)}) collective-permute-start(bf16[768,512]{1,0:T(8,128)(2,1)} %collective-permute-done.3), channel_id=1, source_target_pairs={{3,0},{5,6},{11,8},{13,14},{19,16},{21,22},{27,24},{29,30},{35,32}... | collective-permute-start | bytes 2359304 | tf_op jit(solution)/shard_map/ppermute | solution.py:21
  74.0 9.1 %collective-permute-start.12 = (bf16[96,512]{1,0:T(8,128)(2,1)S(1)}, bf16[96,512]{1,0:T(8,128)(2,1)S(1)}, u32[]{:S(2)}, u32[]{:S(2)}) collective-permute-start(bf16[96,512]{1,0:T(8,128)(2,1)S(1)} %get-tuple-element.12.w0), channel_id=1, source_target_pairs={{1,0},{7,6},{9,8},{15,14},{17,16},{23,22},{25,24},{31,30},{33,32},... | collective-permute-start | bytes 294920 | tf_op jit(solution)/shard_map/ppermute | solution.py:21
  75.9 16.4 %all-to-all-start.1 = ((bf16[16,16,128]{2,1,0:T(8,128)(2,1)}), bf16[16,16,128]{2,1,0:T(8,128)(2,1)S(1)}, u32[]{:S(2)}, u32[]{:S(2)}) async-start(bf16[16,16,128]{2,1,0:T(8,128)(2,1)} %broadcast_in_dim.102), calls=%async_computation.1 | async-start | bytes 131072 | tf_op jit(solution)/shard_map/all_to_all | solution.py:332
  83.1 8.0 %collective-permute-start.13 = (bf16[96,512]{1,0:T(8,128)(2,1)S(1)}, bf16[96,512]{1,0:T(8,128)(2,1)S(1)}, u32[]{:S(2)}, u32[]{:S(2)}) collective-permute-start(bf16[96,512]{1,0:T(8,128)(2,1)S(1)} %get-tuple-element.12.w0), channel_id=1, source_target_pairs={{2,0},{4,6},{10,8},{12,14},{18,16},{20,22},{26,24},{28,30},{34,32}... | collective-permute-start | bytes 294920 | tf_op jit(solution)/shard_map/ppermute | solution.py:21
  91.1 7.7 %collective-permute-start.14 = (bf16[96,512]{1,0:T(8,128)(2,1)S(1)}, bf16[96,512]{1,0:T(8,128)(2,1)S(1)}, u32[]{:S(2)}, u32[]{:S(2)}) collective-permute-start(bf16[96,512]{1,0:T(8,128)(2,1)S(1)} %get-tuple-element.12.w0), channel_id=1, source_target_pairs={{3,0},{5,6},{11,8},{13,14},{19,16},{21,22},{27,24},{29,30},{35,32}... | collective-permute-start | bytes 294920 | tf_op jit(solution)/shard_map/ppermute | solution.py:21
  121.9 4.4 %collective-permute-start.15 = (bf16[32,512]{1,0:T(8,128)(2,1)S(1)}, bf16[32,512]{1,0:T(8,128)(2,1)S(1)}, u32[]{:S(2)}, u32[]{:S(2)}) collective-permute-start(bf16[32,512]{1,0:T(8,128)(2,1)S(1)} %get-tuple-element.27), channel_id=1, source_target_pairs={{0,1},{6,7},{8,9},{14,15},{16,17},{22,23},{24,25},{30,31},{32,33},... | collective-permute-start | bytes 98312 | tf_op jit(solution)/shard_map/ppermute | solution.py:21
  123.2 3.1 %collective-permute-start.16 = (bf16[32,512]{1,0:T(8,128)(2,1)S(1)}, bf16[32,512]{1,0:T(8,128)(2,1)S(1)}, u32[]{:S(2)}, u32[]{:S(2)}) collective-permute-start(bf16[32,512]{1,0:T(8,128)(2,1)S(1)} %get-tuple-element.26), channel_id=1, source_target_pairs={{0,2},{6,4},{8,10},{14,12},{16,18},{22,20},{24,26},{30,28},{32,34}... | collective-permute-start | bytes 98312 | tf_op jit(solution)/shard_map/ppermute | solution.py:21
  124.5 2.9 %collective-permute-start.17 = (bf16[32,512]{1,0:T(8,128)(2,1)S(1)}, bf16[32,512]{1,0:T(8,128)(2,1)S(1)}, u32[]{:S(2)}, u32[]{:S(2)}) collective-permute-start(bf16[32,512]{1,0:T(8,128)(2,1)S(1)} %get-tuple-element.25), channel_id=1, source_target_pairs={{0,3},{6,5},{8,11},{14,13},{16,19},{22,21},{24,27},{30,29},{32,35}... | collective-permute-start | bytes 98312 | tf_op jit(solution)/shard_map/ppermute | solution.py:21
  127.4 1.3 collective-permute-start.18
  129.7 17.3 %all-to-all-start.2 = ((bf16[16,32,512]{2,1,0:T(8,128)(2,1)}), bf16[16,32,512]{2,1,0:T(8,128)(2,1)S(1)}, u32[]{:S(2)}, u32[]{:S(2)}) async-start(bf16[16,32,512]{2,1,0:T(8,128)(2,1)} %select_select_fusion), calls=%async_computation.2 | async-start | bytes 1048576 | tf_op jit(solution)/shard_map/all_to_all | solution.py:348
  147.1 11.9 %collective-permute-start.19 = (bf16[32,512]{1,0:T(8,128)(2,1)S(1)}, bf16[32,512]{1,0:T(8,128)(2,1)S(1)}, u32[]{:S(2)}, u32[]{:S(2)}) collective-permute-start(bf16[32,512]{1,0:T(8,128)(2,1)S(1)} %multiply_convert_fusion.v0), channel_id=1, source_target_pairs={{1,0},{2,1},{3,2},{0,3},{5,4},{6,5},{7,6},{4,7},{9,8},{10,9},{11,1... | collective-permute-start | bytes 98312 | tf_op jit(solution)/shard_map/ppermute | solution.py:32
  150.6 8.3 %collective-permute-start.20 = (bf16[32,512]{1,0:T(8,128)(2,1)S(1)}, bf16[32,512]{1,0:T(8,128)(2,1)S(1)}, u32[]{:S(2)}, u32[]{:S(2)}) collective-permute-start(bf16[32,512]{1,0:T(8,128)(2,1)S(1)} %multiply_convert_fusion.v0), channel_id=1, source_target_pairs={{2,0},{3,1},{0,2},{1,3},{6,4},{7,5},{4,6},{5,7},{10,8},{11,9},{8,1... | collective-permute-start | bytes 98312 | tf_op jit(solution)/shard_map/ppermute | solution.py:32
  150.6 8.3 %collective-permute-start.21 = (bf16[32,512]{1,0:T(8,128)(2,1)S(1)}, bf16[32,512]{1,0:T(8,128)(2,1)S(1)}, u32[]{:S(2)}, u32[]{:S(2)}) collective-permute-start(bf16[32,512]{1,0:T(8,128)(2,1)S(1)} %multiply_convert_fusion.v0), channel_id=1, source_target_pairs={{3,0},{0,1},{1,2},{2,3},{7,4},{4,5},{5,6},{6,7},{11,8},{8,9},{9,10... | collective-permute-start | bytes 98312 | tf_op jit(solution)/shard_map/ppermute | solution.py:32
  162.3 7.6 %collective-permute-start.22 = (f32[96,512]{1,0:T(8,128)S(1)}, f32[96,512]{1,0:T(8,128)S(1)}, u32[]{:S(2)}, u32[]{:S(2)}) collective-permute-start(f32[96,512]{1,0:T(8,128)S(1)} %get-tuple-element.24), channel_id=1, source_target_pairs={{0,1},{6,7},{8,9},{14,15},{16,17},{22,23},{24,25},{30,31},{32,33},... | collective-permute-start | bytes 589832 | tf_op jit(solution)/shard_map/ppermute | solution.py:21
  166.7 5.3 %collective-permute-start.23 = (f32[96,512]{1,0:T(8,128)S(1)}, f32[96,512]{1,0:T(8,128)S(1)}, u32[]{:S(2)}, u32[]{:S(2)}) collective-permute-start(f32[96,512]{1,0:T(8,128)S(1)} %get-tuple-element.23), channel_id=1, source_target_pairs={{0,2},{6,4},{8,10},{14,12},{16,18},{22,20},{24,26},{30,28},{32,34}... | collective-permute-start | bytes 589832 | tf_op jit(solution)/shard_map/ppermute | solution.py:21
  168.1 4.5 %collective-permute-start.24 = (f32[96,512]{1,0:T(8,128)S(1)}, f32[96,512]{1,0:T(8,128)S(1)}, u32[]{:S(2)}, u32[]{:S(2)}) collective-permute-start(f32[96,512]{1,0:T(8,128)S(1)} %get-tuple-element.22), channel_id=1, source_target_pairs={{0,3},{6,5},{8,11},{14,13},{16,19},{22,21},{24,27},{30,29},{32,35}... | collective-permute-start | bytes 589832 | tf_op jit(solution)/shard_map/ppermute | solution.py:21
  (7 other events, 31.5 us)
